TPU v7x, 32 devices: a whole 2x2x4 slice. The times are simulated.
32 devices in a mesh: grp: 2 (over x), seq: 16 (over z, y, core).
Axes of the slice: x: 2, y: 2, z: 4, core: 2. Of those that a mesh axis runs over, the one named last changes fastest.
Arguments:
- llm_grad: bfloat16 [4096, 8192], P('seq', 'grp'), may hold values from -6 to 6
- image_grid: int32 [256, 2], replicated, may hold values from 1 to 3, as said below
- image_owner: int32 [256], replicated, may hold values from 0 to 15, as said below
- row_start: int32 [256], replicated, may hold values from 0 to 255, as said below
- merger_pre: bfloat16 [48, 16, 2560], P(None, 'seq', 'grp'), may hold values from -6 to 6
- vit_out: bfloat16 [192, 16, 1280], P(None, 'seq'), may hold values from -6 to 6
- vit_pre: bfloat16 [192, 16, 2560], P(None, 'seq', 'grp'), may hold values from -6 to 6
- ln_gain: float32 [1280], replicated, may hold values from 0.25 to 1.75
- merger_out_w: bfloat16 [8192, 2560], P('seq', 'grp'), may hold values from -0.0625 to 0.0625
- merger_in_w: bfloat16 [2560, 5120], P('grp', 'seq'), may hold values from -0.125 to 0.125
- vit_fc2_w: bfloat16 [1280, 2560], P('seq', 'grp'), may hold values from -0.15625 to 0.15625
Outputs:
- patch_grad: bfloat16 [192, 16, 1280], P('grp', 'seq')
- fc1_grad: bfloat16 [192, 16, 2560], P(None, 'seq', 'grp')
- fc2_w_grad: float32 [1280, 2560], P('seq', 'grp')
Inputs may be any that keep to these rules, and one draw needn't show every extreme that they name: `image_grid`: height times width is 1 to 3; the first image of every shard is 1 by 3; the last image of shard 0 is 1 by 1. `image_owner`: the 16 images of one shard have 16 different owners. An image's rows row_start to row_start + t - 1 lie inside its shard and meet no other image's rows; a shard's images follow the order of k; the last image of every shard ends at the shard's last row; the first image of shard 0 starts at row 0.
All inputs are finite; a program needn't handle non-finite values.
Results may differ from a plain program's by a relative error of at most 0.02.
Values may be sent and summed in bfloat16 or wider, within the bound.
A program may use at most 128 MiB of HBM per device.

v0:
```python
import jax
import jax.numpy as jnp
from jax import lax
from jax.sharding import PartitionSpec as P

SLOT = 3


def gelu_slope(values):
    return (
        0.5 * (1.0 + lax.erf(values * 0.7071067811865476))
        + values * jnp.exp(-0.5 * values * values) * 0.3989422804014327
    )


def patch_table(widths, counts, slots):
    places = jnp.arange(4 * slots, dtype=jnp.int32)
    merged = places // 4
    corner = places % 4
    row_in = merged[None, :] // widths[:, None]
    col_in = merged[None, :] % widths[:, None]
    target = (
        (2 * row_in + corner[None, :] // 2) * (2 * widths[:, None])
        + 2 * col_in
        + corner[None, :] % 2
    )
    usable = merged[None, :] < counts[:, None]
    return ((target[:, None, :] == places[None, :, None]) & usable[:, None, :]).astype(jnp.float32)


def norm_backward(upstream, inputs, scales):
    average = jnp.mean(inputs, -1, keepdims=True)
    centred = inputs - average
    inverse_std = lax.rsqrt(jnp.mean(centred * centred, -1, keepdims=True) + 1e-06)
    normed = centred * inverse_std
    scaled = upstream * scales
    return inverse_std * (
        scaled
        - jnp.mean(scaled, -1, keepdims=True)
        - normed * jnp.mean(scaled * normed, -1, keepdims=True)
    )


def on_device(
    llm_grad,
    image_grid,
    image_owner,
    row_start,
    merger_pre,
    vit_out,
    vit_pre,
    ln_gain,
    merger_out_w,
    merger_in_w,
    vit_fc2_w,
):
    seq_count = lax.axis_size("seq")
    own_index = lax.axis_index("seq")
    grids = image_grid.reshape(seq_count, seq_count, 2)
    counts = grids[:, :, 0] * grids[:, :, 1]
    widths = grids[:, :, 1]
    owners = image_owner.reshape(seq_count, seq_count)
    starts = row_start.reshape(seq_count, seq_count)
    within = jnp.arange(SLOT, dtype=jnp.int32)
    peers = jnp.arange(seq_count, dtype=jnp.int32)
    shard_rows = llm_grad.shape[0]
    my_owners = lax.dynamic_index_in_dim(owners, own_index, 0, keepdims=False)
    my_counts = lax.dynamic_index_in_dim(counts, own_index, 0, keepdims=False)
    my_starts = lax.dynamic_index_in_dim(starts, own_index, 0, keepdims=False)
    targets = (my_owners[None, :] == peers[:, None]).astype(jnp.int32)
    send_counts = jnp.sum(targets * my_counts[None, :], 1)
    send_starts = jnp.sum(targets * my_starts[None, :], 1)
    indices = jnp.minimum(send_starts[:, None] + within[None, :], shard_rows - 1)
    usable = within[None, :] < send_counts[:, None]
    picked = jnp.take(llm_grad, indices.reshape(-1), axis=0)
    outgoing = jnp.where(usable.reshape(-1, 1), picked, jnp.zeros_like(picked)).reshape(
        seq_count, SLOT, llm_grad.shape[1]
    )
    received = (owners == own_index).astype(jnp.int32)
    recv_counts = jnp.sum(received * counts, 1)
    recv_widths = jnp.sum(received * widths, 1)
    wide_rows = lax.all_gather(
        outgoing.reshape(-1, llm_grad.shape[1]), "grp", axis=1, tiled=True
    )
    sliced = lax.all_to_all(wide_rows, "seq", split_axis=1, concat_axis=0, tiled=True)
    features = sliced.shape[1]
    by_owner = jnp.swapaxes(
        sliced.reshape(seq_count, seq_count, SLOT, features), 0, 1
    ).reshape(-1, features)
    folded = jnp.dot(by_owner, merger_out_w, preferred_element_type=jnp.float32)
    arrived = lax.all_to_all(
        folded.astype(jnp.bfloat16), "seq", split_axis=0, concat_axis=0, tiled=True
    )
    unit_grad = jnp.sum(
        arrived.reshape(seq_count, seq_count * SLOT, -1).astype(jnp.float32), 0
    ).astype(jnp.bfloat16)
    pre_act = merger_pre[:, 0, :].astype(jnp.float32)
    pre_grad = (gelu_slope(pre_act) * unit_grad.astype(jnp.float32)).astype(jnp.bfloat16)
    all_pre = lax.all_gather(pre_grad, "seq", axis=0, tiled=True)
    part_cols = jnp.dot(all_pre, merger_in_w, preferred_element_type=jnp.float32)
    part_rows = lax.all_to_all(
        part_cols.astype(jnp.bfloat16), "seq", split_axis=0, concat_axis=1, tiled=True
    )
    merged_part = jnp.sum(
        lax.all_gather(part_rows, "grp", axis=0).astype(jnp.float32), 0
    )
    vit_width = vit_out.shape[2]
    table = patch_table(recv_widths, recv_counts, SLOT)
    patch_in = jnp.einsum(
        "spq,sqc->spc",
        table,
        merged_part.reshape(seq_count, 4 * SLOT, vit_width),
        precision=lax.Precision.HIGHEST,
    ).reshape(-1, vit_width)
    patch_grad = norm_backward(patch_in, vit_out[:, 0, :].astype(jnp.float32), ln_gain).astype(
        jnp.bfloat16
    )
    group_rows = patch_grad.shape[0] // lax.axis_size("grp")
    own_rows = lax.dynamic_slice_in_dim(
        patch_grad, lax.axis_index("grp") * group_rows, group_rows, 0
    )
    columns = patch_grad
    act_grad = jnp.dot(
        columns,
        lax.all_gather(vit_fc2_w, "seq", axis=0, tiled=True),
        preferred_element_type=jnp.float32,
    )
    fc_in = vit_pre[:, 0, :].astype(jnp.float32)
    sigmoid_q = jax.nn.sigmoid(1.702 * fc_in)
    activation = (fc_in * sigmoid_q).astype(jnp.bfloat16)
    fc1_grad = ((sigmoid_q + 1.702 * fc_in * sigmoid_q * (1.0 - sigmoid_q)) * act_grad).astype(
        jnp.bfloat16
    )
    columns = patch_grad
    weight_part = lax.dot_general(
        columns, activation, (((0,), (0,)), ((), ())), preferred_element_type=jnp.float32
    )
    weight_parts = lax.all_to_all(
        weight_part.astype(jnp.bfloat16), "seq", split_axis=0, concat_axis=0, tiled=True
    )
    weight_grad = jnp.sum(
        weight_parts.reshape(seq_count, -1, weight_part.shape[1]).astype(jnp.float32), 0
    )
    return (
        own_rows.reshape(group_rows, 1, vit_width),
        fc1_grad.reshape(-1, 1, vit_pre.shape[2]),
        weight_grad,
    )


def solution(mesh):
    return jax.shard_map(
        on_device,
        mesh=mesh,
        in_specs=(
            P("seq", "grp"),
            P(),
            P(),
            P(),
            P(None, "seq", "grp"),
            P(None, "seq", None),
            P(None, "seq", "grp"),
            P(),
            P("seq", "grp"),
            P("grp", "seq"),
            P("seq", "grp"),
        ),
        out_specs=(P("grp", "seq", None), P(None, "seq", "grp"), P("seq", "grp")),
        check_vma=False,
    )
```

profile of v0, /device:TPU:27, one launch (start us, length us, event | category | flops | bytes accessed | tf_op | source)
XLA Modules:
  0.0 291.7 jit_solution(5290898509459888009)
XLA Ops:
  7.2 0.9 reshape.493
  8.9 0.8 reshape.494
  10.4 0.8 gather_fusion
  11.3 10.7 %all_gather.15 = bf16[48,8192]{1,0:T(8,128)(2,1)S(1)} all-gather(bf16[48,4096]{1,0:T(8,128)(2,1)S(1)} %select_select_fusion), channel_id=1, replica_groups=mesh['grp'=2,'seq'=16] {'grp'}, dimensions={1}, use_global_device_ids=true | all-gather | bytes 1179648 | tf_op jit(solution)/shard_map/all_gather | solution.py:82
  22.1 25.8 %all_to_all.50 = bf16[48,16,512]{2,0,1:T(8,128)(2,1)S(1)} all-to-all(bf16[48,16,512]{2,0,1:T(8,128)(2,1)S(1)} %bitcast.84), channel_id=1, replica_groups=mesh['grp'=2,'seq'=16] {'seq'}, dimensions={1} | all-to-all | bytes 1572864 | tf_op jit(solution)/shard_map/all_to_all | solution.py:85
  49.0 1.4 reshape.497
  50.5 2.7 convolution_convert_fusion.1
  53.2 49.0 %all_to_all.51 = bf16[16,48,1280]{2,1,0:T(8,128)(2,1)} all-to-all(bf16[16,48,1280]{2,1,0:T(8,128)(2,1)S(1)} %bitcast.85), channel_id=1, replica_groups=mesh['grp'=2,'seq'=16] {'seq'}, dimensions={0} | all-to-all | bytes 3932160 | tf_op jit(solution)/shard_map/all_to_all | solution.py:91
  102.2 1.9 reduce_sum.108
  104.1 0.8 fusion.26
  106.1 39.4 %all-gather.3.cloned.1.call-done = bf16[768,1280]{1,0:T(8,128)(2,1)} async-done(((bf16[48,1280]{1,0:T(8,128)(2,1)}), bf16[768,1280]{1,0:T(8,128)(2,1)}) %all-gather.3.cloned.1.call-update) | async-done | bytes 1966096 | tf_op jit(solution)/shard_map/all_gather | solution.py:99
  145.5 2.6 convolution_convert_fusion.2
  148.1 1.1 copy.22
  149.1 5.7 %all-to-all-start.2 = ((bf16[16,48,320]{2,1,0:T(8,128)(2,1)}), bf16[16,48,320]{2,1,0:T(8,128)(2,1)}, u32[]{:S(2)}, u32[]{:S(2)}) async-start(bf16[16,48,320]{2,1,0:T(8,128)(2,1)} %bitcast.13), calls=%async_computation.2 | async-start | bytes 1179648 | tf_op jit(solution)/shard_map/all_to_all | solution.py:101
  154.9 1.1 reshape.503
  156.5 18.8 %all-to-all-done.2 = bf16[16,48,320]{2,1,0:T(8,128)(2,1)} async-done(((bf16[16,48,320]{2,1,0:T(8,128)(2,1)}), bf16[16,48,320]{2,1,0:T(8,128)(2,1)}, u32[]{:S(2)}, u32[]{:S(2)}) %all-to-all-start.2) | async-done | bytes 491552 | tf_op jit(solution)/shard_map/all_to_all | solution.py:101
  175.3 2.0 copy.23
  177.3 2.3 all_gather.17
  179.6 14.0 %all_gather.18 = bf16[2,48,5120]{2,1,0:T(8,128)(2,1)S(1)} all-gather(bf16[1,48,5120]{2,1,0:T(8,128)(2,1)} %all_gather.17), channel_id=1, replica_groups=mesh['grp'=2,'seq'=16] {'grp'}, dimensions={0}, use_global_device_ids=true | all-gather | bytes 1474560 | tf_op jit(solution)/shard_map/all_gather | solution.py:105
  193.6 1.1 convert_reduce_fusion.1
  194.7 2.5 reshape.498
  197.3 2.4 multiply_reduce_fusion.1
  199.8 1.1 copy-done.1
  200.8 1.3 multiply_convert_fusion
  202.1 1.2 convert_element_type.82
  203.3 3.9 %convolution_convert_fusion = bf16[1280,1280]{1,0:T(8,128)(2,1)} fusion(bf16[192,1280]{1,0:T(8,128)(2,1)S(1)} %convert_element_type.82, bf16[192,1,1280]{2,0,1:T(8,128)(2,1)} %param.17), kind=kOutput, calls=%fused_computation.1 | convolution fusion | flops 632504320 | bytes 4259840 | tf_op jit(solution)/shard_map/dot_general | solution.py:135
  207.1 6.5 %all-to-all-start.3 = ((bf16[16,80,1280]{2,1,0:T(8,128)(2,1)}), bf16[16,80,1280]{2,1,0:T(8,128)(2,1)}, u32[]{:S(2)}, u32[]{:S(2)}) async-start(bf16[16,80,1280]{2,1,0:T(8,128)(2,1)} %bitcast.81), calls=%async_computation.3 | async-start | bytes 6553600 | tf_op jit(solution)/shard_map/all_to_all | solution.py:138
  213.7 1.1 reshape.499
  214.9 1.7 multiply_convert_fusion.1
  217.3 3.6 %fusion.1 = bf16[192,1,1280]{2,0,1:T(8,128)(2,1)} fusion(bf16[192,1280]{1,0:T(8,128)(2,1)S(1)} %multiply_convert_fusion.1, bf16[1280,1280]{1,0:T(8,128)(2,1)} %all-gather.5.cloned.1.call-done, bf16[192,1,1280]{2,0,1:T(8,128)(2,1)S(1)} %copy-done.6), kind=kOutput, calls=%fused_computation.6 | convolution fusion | flops 631848960 | bytes 4751360 | tf_op jit(solution)/shard_map/dot_general | solution.py:123
  220.9 60.7 %all-to-all-done.3 = bf16[16,80,1280]{2,1,0:T(8,128)(2,1)} async-done(((bf16[16,80,1280]{2,1,0:T(8,128)(2,1)}), bf16[16,80,1280]{2,1,0:T(8,128)(2,1)}, u32[]{:S(2)}, u32[]{:S(2)}) %all-to-all-start.3) | async-done | bytes 3276832 | tf_op jit(solution)/shard_map/all_to_all | solution.py:138
  281.6 3.2 %convert_reduce_fusion = f32[80,1280]{1,0:T(8,128)} fusion(bf16[16,80,1280]{2,1,0:T(8,128)(2,1)} %all-to-all-done.3), kind=kLoop, calls=%fused_computation.2 | loop fusion | flops 3174400 | bytes 3686400 | tf_op jit(solution)/shard_map/reduce_sum | solution.py:141
  (52 shorter events, 5.4 us)
Async XLA Ops:
  7.2 3.2 %copy-start = (bf16[256,4096]{1,0:T(8,128)(2,1)S(1)}, bf16[256,4096]{1,0:T(8,128)(2,1)}, u32[]{:S(2)}) copy-start(bf16[256,4096]{1,0:T(8,128)(2,1)} %param.11) | copy-start | bytes 6291460
  7.2 138.3 %all-gather.3.cloned.1.call-start = ((), (), s32[]{:S(2)}) async-start(), calls=%async_computation.4 | async-start | bytes 2088960 | tf_op jit(solution)/shard_map/all_gather | solution.py:99
  102.2 1.9 copy-start.4
  102.2 3.5 %copy-start.3 = (bf16[192,1,1280]{2,0,1:T(8,128)(2,1)S(1)}, bf16[192,1,1280]{2,0,1:T(8,128)(2,1)}, u32[]{:S(2)}) copy-start(bf16[192,1,1280]{2,0,1:T(8,128)(2,1)} %param.16) | copy-start | bytes 1474564
  104.9 112.4 %all-gather.5.cloned.1.call-start = ((), (), s32[]{:S(2)}) async-start(), calls=%async_computation.5 | async-start | bytes 3481600 | tf_op jit(solution)/shard_map/all_gather | solution.py:125
  149.1 26.2 %all-to-all-start.2 = ((bf16[16,48,320]{2,1,0:T(8,128)(2,1)}), bf16[16,48,320]{2,1,0:T(8,128)(2,1)}, u32[]{:S(2)}, u32[]{:S(2)}) async-start(bf16[16,48,320]{2,1,0:T(8,128)(2,1)} %bitcast.13), calls=%async_computation.2 | async-start | bytes 1179648 | tf_op jit(solution)/shard_map/all_to_all | solution.py:101
  194.7 2.6 copy-start.5
  199.7 1.1 copy-start.1
  207.1 6.6 %copy-start.2 = (f32[16,12,1280]{2,1,0:T(8,128)S(1)}, f32[16,12,1280]{2,1,0:T(8,128)}, u32[]{:S(2)}) copy-start(f32[16,12,1280]{2,1,0:T(8,128)} %copy-done.1) | copy-start | bytes 2949124
  207.1 74.5 %all-to-all-start.3 = ((bf16[16,80,1280]{2,1,0:T(8,128)(2,1)}), bf16[16,80,1280]{2,1,0:T(8,128)(2,1)}, u32[]{:S(2)}, u32[]{:S(2)}) async-start(bf16[16,80,1280]{2,1,0:T(8,128)(2,1)} %bitcast.81), calls=%async_computation.3 | async-start | bytes 6553600 | tf_op jit(solution)/shard_map/all_to_all | solution.py:138
  214.8 2.5 copy-start.6
Sparse Core Ops, SparseCore 0:
  105.0 40.4 all-gather.2
  147.8 50.6 all-gather.4
where the time goes:
time: 298 us; the launch traced here: 292 us
  waiting for transfers between devices  120 us (40%)
  blocking collectives  99.5 us (33%)
  local copies, waits for them, and re-layouts  19.6 us (7%)
  matrix products  15.2 us (5%)
  between operations  14.3 us (5%)
  starting transfers between devices  12.2 us (4%)
  other arithmetic  11.3 us (4%)
    all_to_all x1, waiting for transfers between devices, on_device(): lax.all_to_all(weight_part.astype(jnp.bfloat16), 'seq', split_axis=0, con...  60.7 us
    all_to_all x1, blocking collectives, on_device(): lax.all_to_all(folded.astype(jnp.bfloat16), 'seq', split_axis=0, concat_a...  49 us
    all_gather x1, waiting for transfers between devices, on_device(): all_pre = lax.all_gather(pre_grad, 'seq', axis=0, tiled=True)  39.4 us
    all_to_all x1, blocking collectives, on_device(): lax.all_to_all(wide_rows, 'seq', split_axis=1, concat_axis=0, tiled=True)  25.8 us
    all_to_all x1, waiting for transfers between devices, on_device(): lax.all_to_all(part_cols.astype(jnp.bfloat16), 'seq', split_axis=0, conca...  18.8 us
    all_gather x1, blocking collectives, on_device(): lax.all_gather(part_rows, 'grp', axis=0).astype(jnp.float32)  14 us
    all_gather x1, blocking collectives, on_device(): lax.all_gather(outgoing.reshape(-1, llm_grad.shape[1]), 'grp', axis=1, ti...  10.7 us
    all_to_all x1, starting transfers between devices, on_device(): lax.all_to_all(weight_part.astype(jnp.bfloat16), 'seq', split_axis=0, con...  6.46 us
  transfers between devices with their start and end apart: 4, of which 3 were waited for; matrix products, arithmetic and copies ran while one was open for 9% of the time, Pallas kernels for 0%

commit v1 on v0

--- a/solution.py
+++ b/solution.py
@@ -1,9 +1,16 @@
+import functools
+
 import jax
 import jax.numpy as jnp
 from jax import lax
+from jax.experimental import pallas as pl
+from jax.experimental.pallas import tpu as pltpu
 from jax.sharding import PartitionSpec as P
 
 SLOT = 3
+MESH = pl.DeviceIdType.MESH
+F32 = jnp.float32
+BF16 = jnp.bfloat16
 
 
 def gelu_slope(values):
@@ -119,9 +126,8 @@
     own_rows = lax.dynamic_slice_in_dim(
         patch_grad, lax.axis_index("grp") * group_rows, group_rows, 0
     )
-    columns = patch_grad
     act_grad = jnp.dot(
-        columns,
+        patch_grad,
         lax.all_gather(vit_fc2_w, "seq", axis=0, tiled=True),
         preferred_element_type=jnp.float32,
     )
@@ -131,9 +137,8 @@
     fc1_grad = ((sigmoid_q + 1.702 * fc_in * sigmoid_q * (1.0 - sigmoid_q)) * act_grad).astype(
         jnp.bfloat16
     )
-    columns = patch_grad
     weight_part = lax.dot_general(
-        columns, activation, (((0,), (0,)), ((), ())), preferred_element_type=jnp.float32
+        patch_grad, activation, (((0,), (0,)), ((), ())), preferred_element_type=jnp.float32
     )
     weight_parts = lax.all_to_all(
         weight_part.astype(jnp.bfloat16), "seq", split_axis=0, concat_axis=0, tiled=True
@@ -148,9 +153,637 @@
     )
 
 
+def small_div(values, by):
+    return (values * ((65536 + by - 1) // by)) >> 16
+
+
+def iota(shape, dim):
+    return lax.broadcasted_iota(jnp.int32, shape, dim)
+
+
+def sum_where(mask, values):
+    return jnp.sum(jnp.where(mask, values, 0.0), 1, keepdims=True).astype(jnp.int32)
+
+
+def fused_kernel(
+    n_grp,
+    n_seq,
+    llm,
+    grid,
+    owner,
+    start,
+    mpre,
+    vout,
+    vpre,
+    gain,
+    wout,
+    win,
+    fc2,
+    pg_out,
+    fc1_out,
+    wg_out,
+    llm_v,
+    mpre_v,
+    vout_v,
+    vpre_v,
+    wo,
+    wi2,
+    wi,
+    wf,
+    act,
+    fslope,
+    gslope,
+    rows_all,
+    xin,
+    xflat,
+    xperm,
+    ys,
+    own1,
+    ry,
+    zs,
+    rz,
+    allp,
+    p2,
+    xs,
+    own2,
+    rx,
+    a2s,
+    mg,
+    m4,
+    pgall,
+    fc1_v,
+    own3,
+    y3s,
+    ry3,
+    z3s,
+    rz3,
+    wg_v,
+    ld_sem,
+    out_sem,
+    send_sem,
+    xw_sem,
+    xag_sem,
+    xin_sem,
+    ry_sem,
+    rz_sem,
+    agz_sem,
+    agy_sem,
+    rx_sem,
+    mg_sem,
+    fz_sem,
+    fy_sem,
+    fc_sem,
+    pg_sem,
+    ry3_sem,
+    rz3_sem,
+):
+    g = lax.axis_index("grp")
+    s = lax.axis_index("seq")
+    nz = n_seq // 4
+    nq = n_seq // 2
+    z = s // 4
+    y = (s // 2) % 2
+    c = s % 2
+    q = z * 2 + y
+    rows = n_seq * SLOT
+    half = rows // 2
+    tok, feat = llm.shape
+    kc = 2 * wout.shape[0]
+    hid = wout.shape[1]
+    cw = win.shape[1]
+    cc = 2 * cw
+    vit = vout.shape[1]
+    pslot = vout.shape[0]
+    phalf = pslot // 2
+    fw = fc2.shape[0]
+    n_img = owner.shape[1]
+    qg = feat // kc
+    nt = 256
+    fhalf = vit // 2
+
+    def dev(gg, zz, yy, c2):
+        return (gg, (zz * 2 + yy) * 2 + c2)
+
+    x_peer = dev(1 - g, z, y, c)
+    y_peer = dev(g, z, 1 - y, c)
+    c_peer = dev(g, z, y, 1 - c)
+
+    sends = []
+
+    def remote(src, dst, rsem, device):
+        cp = pltpu.make_async_remote_copy(
+            src_ref=src,
+            dst_ref=dst,
+            send_sem=send_sem.at[len(sends)],
+            recv_sem=rsem,
+            device_id=device,
+            device_id_type=MESH,
+        )
+        sends.append(cp)
+        return cp
+
+    def arrive(dst, rsem):
+        pltpu.make_async_copy(dst, dst, rsem).wait()
+
+    barrier = pltpu.get_barrier_semaphore()
+
+    @pl.loop(0, n_grp * n_seq)
+    def _(i):
+        @pl.when(i != g * n_seq + s)
+        def _():
+            pl.semaphore_signal(
+                barrier, inc=1, device_id=(i // n_seq, i % n_seq), device_id_type=MESH
+            )
+
+    loads = {}
+
+    def load(name, src, dst):
+        cp = pltpu.make_async_copy(src, dst, ld_sem.at[len(loads)])
+        cp.start()
+        loads[name] = cp
+
+    for i in range(qg):
+        load(("llm", i), llm.at[:, pl.ds(i * kc, kc)], llm_v.at[:, pl.ds(i * kc, kc)])
+    load("vpre", vpre, vpre_v)
+    load("mpre", mpre, mpre_v)
+    wo_own = wo.at[pl.ds(pl.multiple_of(c * (kc // 2), 16), kc // 2)]
+    load("wo", wout, wo_own)
+    load("wi", win, wi2.at[c])
+    load("wf", fc2, wf.at[s])
+    load("vout", vout.at[pl.ds(pl.multiple_of(g * phalf, 16), phalf)], vout_v)
+
+    r = iota((rows, 1), 0)
+    par = small_div(r, half)
+    rem = r - par * half
+    o2 = small_div(rem, SLOT)
+    slot = rem - o2 * SLOT
+    img = iota((1, n_img), 1)
+    shard_of = small_div(img, n_seq)
+    count = (grid[0:1, :] * grid[1:2, :]).astype(F32)
+    width = grid[1:2, :].astype(F32)
+    starts = start[...].astype(F32)
+    owners = owner[...]
+    mine = (owners == o2 * 2 + par) & (shard_of == s)
+    first = sum_where(mine, jnp.broadcast_to(starts, mine.shape))
+    many = sum_where(mine, jnp.broadcast_to(count, mine.shape))
+    onehot = ((iota((rows, tok), 1) == first + slot) & (slot < many)).astype(BF16)
+
+    for i in range(qg):
+        loads[("llm", i)].wait()
+        picked = jnp.dot(
+            onehot, llm_v[:, i * kc : (i + 1) * kc], preferred_element_type=F32
+        ).astype(BF16)
+        rows_all[g * qg + i, 0] = picked[:half]
+        rows_all[g * qg + i, 1] = picked[half:]
+
+    pl.semaphore_wait(barrier, n_grp * n_seq - 1)
+
+    xag = []
+    for i in range(qg):
+        blk = g * qg + i
+        cp = remote(rows_all.at[blk], rows_all.at[blk], xag_sem.at[i], x_peer)
+        cp.start()
+        xag.append(cp)
+
+    def is_self(qq, p):
+        return (qq == q) & (p == c)
+
+    selfs = []
+
+    def send_rows(qq, p):
+        src = rows_all.at[qq, p]
+        cp = remote(src, xin.at[s], xin_sem.at[s], (g, qq * 2 + p))
+        me = is_self(qq, p)
+        local = pltpu.make_async_copy(src, xin.at[s], xin_sem.at[s])
+
+        @pl.when(jnp.logical_not(me))
+        def _():
+            cp.start()
+
+        @pl.when(me)
+        def _():
+            local.start()
+
+        sends.pop()
+        sends.append((cp, me))
+
+    for i in range(qg):
+        for p in range(2):
+            send_rows(g * qg + i, p)
+
+    remote(wout, wo_own, xw_sem.at[0], c_peer).start()
+    remote(win, wi2.at[c], xw_sem.at[1], c_peer).start()
+
+    for i in range(qg):
+        arrive(rows_all.at[(1 - g) * qg + i], xag_sem.at[i])
+        for p in range(2):
+            send_rows((1 - g) * qg + i, p)
+
+    loads["vpre"].wait()
+    tile = 64 if pslot % 64 == 0 else 16
+
+    @pl.loop(0, pslot // tile)
+    def _(i):
+        sl = pl.ds(pl.multiple_of(i * tile, tile), tile)
+        v = vpre_v[sl, :].astype(F32)
+        sq = jax.nn.sigmoid(1.702 * v)
+        act[c, sl, :] = (v * sq).astype(BF16)
+        fslope[sl, :] = sq + 1.702 * v * sq * (1.0 - sq)
+
+    remote(act.at[c], act.at[c], xw_sem.at[2], c_peer).start()
+    loads["mpre"].wait()
+    gslope[...] = gelu_slope(mpre_v[...].astype(F32))
+
+    r = iota((half * n_seq, 1), 0)
+    oo = small_div(r, rows)
+    rem = r - oo * rows
+    src_s = small_div(rem, SLOT)
+    slot = rem - src_s * SLOT
+    yo = small_div(oo, nz)
+    zo = oo - yo * nz
+    want = src_s * half + (zo * 2 + yo) * SLOT + slot
+    perm = (iota((half * n_seq, half * n_seq), 1) == want).astype(BF16)
+
+    loads["wi"].wait()
+    arrive(wi2.at[1 - c], xw_sem.at[1])
+    wi[...] = jnp.concatenate([wi2[0], wi2[1]], axis=1)
+    loads["wo"].wait()
+    arrive(wo.at[pl.ds(pl.multiple_of((1 - c) * (kc // 2), 16), kc // 2)], xw_sem.at[0])
+
+    for src in range(n_seq):
+        arrive(xin.at[src], xin_sem.at[src])
+        xflat[src * half : (src + 1) * half, :] = xin[src].astype(F32)
+
+    @pl.loop(0, kc // nt)
+    def _(t):
+        sl = pl.ds(pl.multiple_of(t * nt, nt), nt)
+        xperm[:, sl] = jnp.dot(
+            perm, xflat[:, sl].astype(BF16), preferred_element_type=F32
+        ).astype(BF16)
+
+    hrows = nz * rows
+
+    def part1(yy, out):
+        lhs = xperm[pl.ds(pl.multiple_of(yy * hrows, 16), hrows), :]
+
+        @pl.loop(0, hid // nt)
+        def _(t):
+            sl = pl.ds(pl.multiple_of(t * nt, nt), nt)
+            got = jnp.dot(lhs, wo[:, sl], preferred_element_type=F32)
+            for zz in range(nz):
+                out[zz, :, sl] = got[zz * rows : (zz + 1) * rows].astype(out.dtype)
+
+    part1(1 - y, ys)
+    order = [d for d in range(1, nz)] + [0]
+    for d in order:
+        zz = (z + d) % nz
+        remote(ys.at[zz], ry.at[zz], ry_sem.at[d], y_peer).start()
+    part1(y, own1)
+    for d in order:
+        zz = (z + d) % nz
+        arrive(ry.at[zz], ry_sem.at[d])
+        total = own1[zz] + ry[zz].astype(F32)
+        if d:
+            zs[d] = total.astype(BF16)
+            remote(zs.at[d], rz.at[d], rz_sem.at[d], dev(g, zz, y, c)).start()
+        else:
+            unit = total
+    for d in range(1, nz):
+        arrive(rz.at[d], rz_sem.at[d])
+        unit = unit + rz[d].astype(F32)
+    pre = (gslope[...] * unit.astype(BF16).astype(F32)).astype(BF16)
+    allp[q] = pre
+
+    remote(allp.at[q], allp.at[q], agy_sem.at[0], y_peer).start()
+    for d in range(1, nz):
+        remote(allp.at[q], allp.at[q], agz_sem.at[d], dev(g, (z + d) % nz, y, c)).start()
+    for d in range(1, nz):
+        qq = ((z + nz - d) % nz) * 2 + y
+        arrive(allp.at[qq], agz_sem.at[d])
+        remote(allp.at[qq], allp.at[qq], agy_sem.at[d], y_peer).start()
+
+    for d in range(nz):
+        zz = (z + nz - d) % nz
+        arrive(allp.at[zz * 2 + 1 - y], agy_sem.at[d])
+        for yo in range(2):
+            p2[yo * rows : (yo + 1) * rows, :] = jnp.dot(
+                allp[zz * 2 + yo], wi[...], preferred_element_type=F32
+            )
+        for e in range(2):
+            yo = y + e - 2 * y * e
+            far = pl.ds(pl.multiple_of(yo * rows + (1 - g) * half, 8), half)
+            near = pl.ds(pl.multiple_of(yo * rows + g * half, 8), half)
+            xs[d, e] = p2[far, :].astype(BF16)
+            own2[d, e] = p2[near, :].astype(BF16)
+        remote(xs.at[d], rx.at[d], rx_sem.at[d], x_peer).start()
+
+    loads["wf"].wait()
+    for d in range(1, nz):
+        remote(wf.at[s], wf.at[s], fz_sem.at[d], dev(g, (z + d) % nz, y, c)).start()
+    remote(wf.at[s], wf.at[s], fy_sem.at[0], y_peer).start()
+    remote(wf.at[s], wf.at[s], fc_sem.at[0, 0], c_peer).start()
+
+    for d in range(nz):
+        zz = (z + nz - d) % nz
+        arrive(rx.at[d], rx_sem.at[d])
+        for e in range(2):
+            yo = y + e - 2 * y * e
+            total = (own2[d, e].astype(F32) + rx[d, e].astype(F32)).astype(BF16)
+            if d == 0 and e == 0:
+                mg[q] = total
+            else:
+                a2s[d, e] = total
+                remote(a2s.at[d, e], mg.at[q], mg_sem.at[q], dev(g, zz, yo, c)).start()
+
+    for d in range(1, nz):
+        blk = wf.at[dev(g, (z + nz - d) % nz, y, c)[1]]
+        arrive(blk, fz_sem.at[d])
+        remote(blk, blk, fy_sem.at[d], y_peer).start()
+        remote(blk, blk, fc_sem.at[0, d], c_peer).start()
+
+    shape = (phalf, phalf)
+    r = iota((phalf, 1), 0)
+    src_r = small_div(r, 4 * SLOT)
+    place = r - src_r * (4 * SLOT)
+    mine = (owners == s) & (shard_of == src_r + g * (n_seq // 2))
+    many = sum_where(mine, jnp.broadcast_to(count, mine.shape))
+    wide = sum_where(mine, jnp.broadcast_to(width, mine.shape))
+    col = iota(shape, 1)
+    comp = small_div(col, half)
+    rem = col - comp * half
+    src_c = small_div(rem, SLOT)
+    slot = rem - src_c * SLOT
+    row_in = jnp.zeros(shape, jnp.int32)
+    for k in range(1, SLOT):
+        row_in = row_in + (slot >= k * wide).astype(jnp.int32)
+    col_in = slot - row_in * wide
+    upper = comp >> 1
+    target = (2 * row_in + upper) * (2 * wide) + 2 * col_in + (comp - 2 * upper)
+    table = ((src_c == src_r) & (slot < many) & (target == place)).astype(BF16)
+    loads["vout"].wait()
+
+    per = vit // cc
+    for qq in range(nq):
+
+        @pl.when(qq != q)
+        def _():
+            arrive(mg.at[qq], mg_sem.at[qq])
+
+        part, piece = qq // per, qq % per
+        m4[part * half : (part + 1) * half, piece * cc : (piece + 1) * cc] = mg[qq].astype(F32)
+    patch_in = jnp.dot(table, m4[...].astype(BF16), preferred_element_type=F32)
+    pg = norm_backward(patch_in, vout_v[...].astype(F32), gain[...]).astype(BF16)
+    own_rows = pgall.at[c, g]
+    pgall[c, g] = pg
+    remote(own_rows, own_rows, pg_sem.at[0], x_peer).start()
+    remote(own_rows, own_rows, pg_sem.at[1], c_peer).start()
+    put_pg = pltpu.make_async_copy(own_rows, pg_out, out_sem.at[0])
+    put_pg.start()
+
+    for d in range(nz):
+        blk = wf.at[dev(g, (z + nz - d) % nz, 1 - y, c)[1]]
+        arrive(blk, fy_sem.at[d])
+        remote(blk, blk, fc_sem.at[1, d], c_peer).start()
+
+    far_rows = pgall.at[c, 1 - g]
+    arrive(far_rows, pg_sem.at[0])
+    remote(far_rows, far_rows, pg_sem.at[2], c_peer).start()
+    arrive(act.at[1 - c], xw_sem.at[2])
+    arrive(pgall.at[1 - c, g], pg_sem.at[1])
+    arrive(pgall.at[1 - c, 1 - g], pg_sem.at[2])
+
+    lane = pl.multiple_of(c * fhalf, 128)
+    quarter = 2 * fw
+    zh = nz // 2
+    lhs = [
+        pgall[i, j, :, pl.ds(lane, fhalf)].T for i in range(2) for j in range(2)
+    ]
+    lhs = jnp.concatenate(lhs, axis=1)
+    own3[...] = jnp.dot(
+        lhs, jnp.concatenate([act[0], act[1]], axis=0), preferred_element_type=F32
+    )
+    for zz in range(zh):
+        base = pl.multiple_of((zz * 2 + 1 - y) * quarter, 16)
+        for c2 in range(2):
+            y3s[zz, c2] = own3[pl.ds(base + c2 * fw, fw), :].astype(BF16)
+            remote(y3s.at[zz, c2], ry3.at[zz, c2], ry3_sem.at[zz, c2], y_peer).start()
+    for zz in range(zh):
+        base = pl.multiple_of((zz * 2 + y) * quarter, 16)
+        for c2 in range(2):
+            arrive(ry3.at[zz, c2], ry3_sem.at[zz, c2])
+            total = own3[pl.ds(base + c2 * fw, fw), :] + ry3[zz, c2].astype(F32)
+            to_z = c * zh + zz
+            me = (to_z == z) & (c2 == c)
+            z3s[zz, c2] = total.astype(BF16)
+            cp = remote(z3s.at[zz, c2], rz3.at[z], rz3_sem.at[z], dev(g, to_z, y, c2))
+
+            @pl.when(me)
+            def _():
+                rz3[z] = total.astype(BF16)
+
+            @pl.when(jnp.logical_not(me))
+            def _():
+                cp.start()
+
+            sends.pop()
+            sends.append((cp, me))
+
+    for d in range(nz):
+        for e in range(2):
+            yy = y + e - 2 * y * e
+            arrive(wf.at[dev(g, (z + nz - d) % nz, yy, 1 - c)[1]], fc_sem.at[e, d])
+    own_pg = jnp.concatenate([pgall[c, 0], pgall[c, 1]], axis=0)
+    wfull = wf.reshape(vit, hid)
+
+    @pl.loop(0, hid // nt)
+    def _(t):
+        sl = pl.ds(pl.multiple_of(t * nt, nt), nt)
+        got = jnp.dot(own_pg, wfull[:, sl], preferred_element_type=F32)
+        fc1_v[:, sl] = (fslope[:, sl] * got).astype(BF16)
+
+    put_fc1 = pltpu.make_async_copy(fc1_v, fc1_out, out_sem.at[1])
+    put_fc1.start()
+
+    total = jnp.zeros((fw, hid), F32)
+    for zz in range(nz):
+
+        @pl.when(jnp.logical_not((zz == z) & (c == z // zh)))
+        def _():
+            arrive(rz3.at[zz], rz3_sem.at[zz])
+
+        total = total + rz3[zz].astype(F32)
+    wg_v[...] = total
+    put_wg = pltpu.make_async_copy(wg_v, wg_out, out_sem.at[2])
+    put_wg.start()
+
+    for item in sends:
+        if isinstance(item, tuple):
+            cp, me = item
+
+            @pl.when(jnp.logical_not(me))
+            def _():
+                cp.wait_send()
+
+        else:
+            item.wait_send()
+    put_pg.wait()
+    put_fc1.wait()
+    put_wg.wait()
+
+
+def fused_on_device(
+    llm_grad,
+    image_grid,
+    image_owner,
+    row_start,
+    merger_pre,
+    vit_out,
+    vit_pre,
+    ln_gain,
+    merger_out_w,
+    merger_in_w,
+    vit_fc2_w,
+    *,
+    n_grp,
+    n_seq,
+):
+    n_img = image_owner.shape[0]
+    tok, feat = llm_grad.shape
+    kb, hid = merger_out_w.shape
+    cw = merger_in_w.shape[1]
+    pslot, _, vit = vit_out.shape
+    fw = vit_fc2_w.shape[0]
+    rows = merger_pre.shape[0]
+    half, phalf = rows // 2, pslot // 2
+    nz, nq, kc, cc = n_seq // 4, n_seq // 2, 2 * kb, 2 * cw
+    qg = feat // kc
+    vmem, anyspace = pltpu.VMEM, pl.BlockSpec(memory_space=pl.ANY)
+    vspec = pl.BlockSpec(memory_space=pltpu.VMEM)
+    dma = pltpu.SemaphoreType.DMA
+    scratch = [
+        vmem((tok, feat), BF16),
+        vmem((rows, hid), BF16),
+        vmem((phalf, vit), BF16),
+        vmem((pslot, hid), BF16),
+        vmem((kc, hid), BF16),
+        vmem((2, hid, cw), BF16),
+        vmem((hid, cc), BF16),
+        vmem((n_seq, fw, hid), BF16),
+        vmem((2, pslot, hid), BF16),
+        vmem((pslot, hid), F32),
+        vmem((rows, hid), F32),
+        vmem((nq, 2, half, kc), BF16),
+        vmem((n_seq, half, kc), BF16),
+        vmem((n_seq * half, kc), F32),
+        vmem((n_seq * half, kc), BF16),
+        vmem((nz, rows, hid), BF16),
+        vmem((nz, rows, hid), F32),
+        vmem((nz, rows, hid), BF16),
+        vmem((nz, rows, hid), BF16),
+        vmem((nz, rows, hid), BF16),
+        vmem((nq, rows, hid), BF16),
+        vmem((2 * rows, cc), F32),
+        vmem((nz, 2, half, cc), BF16),
+        vmem((nz, 2, half, cc), BF16),
+        vmem((nz, 2, half, cc), BF16),
+        vmem((nz, 2, half, cc), BF16),
+        vmem((nq, half, cc), BF16),
+        vmem((phalf, vit), F32),
+        vmem((2, 2, phalf, vit), BF16),
+        vmem((pslot, hid), BF16),
+        vmem((vit // 2, hid), F32),
+        vmem((nz // 2, 2, fw, hid), BF16),
+        vmem((nz // 2, 2, fw, hid), BF16),
+        vmem((nz // 2, 2, fw, hid), BF16),
+        vmem((nz, fw, hid), BF16),
+        vmem((fw, hid), F32),
+        dma((qg + 6,)),
+        dma((3,)),
+        dma((256,)),
+        dma((3,)),
+        dma((qg,)),
+        dma((n_seq,)),
+        dma((nz,)),
+        dma((nz,)),
+        dma((nz,)),
+        dma((nz,)),
+        dma((nz,)),
+        dma((nq,)),
+        dma((nz,)),
+        dma((nz,)),
+        dma((2, nz)),
+        dma((3,)),
+        dma((nz // 2, 2)),
+        dma((nz,)),
+    ]
+    pg, fc1, wg = pl.pallas_call(
+        functools.partial(fused_kernel, n_grp, n_seq),
+        out_shape=(
+            jax.ShapeDtypeStruct((phalf, vit), BF16),
+            jax.ShapeDtypeStruct((pslot, hid), BF16),
+            jax.ShapeDtypeStruct((fw, hid), F32),
+        ),
+        in_specs=[
+            anyspace,
+            vspec,
+            vspec,
+            vspec,
+            anyspace,
+            anyspace,
+            anyspace,
+            vspec,
+            anyspace,
+            anyspace,
+            anyspace,
+        ],
+        out_specs=(anyspace, anyspace, anyspace),
+        scratch_shapes=scratch,
+        compiler_params=pltpu.CompilerParams(
+            collective_id=0, has_side_effects=True, vmem_limit_bytes=60 * 1024 * 1024
+        ),
+    )(
+        llm_grad,
+        image_grid.T,
+        image_owner.reshape(1, n_img),
+        row_start.reshape(1, n_img),
+        merger_pre.reshape(rows, hid),
+        vit_out.reshape(pslot, vit),
+        vit_pre.reshape(pslot, hid),
+        ln_gain.reshape(1, vit),
+        merger_out_w,
+        merger_in_w,
+        vit_fc2_w,
+    )
+    return pg.reshape(phalf, 1, vit), fc1.reshape(pslot, 1, hid), wg
+
+
 def solution(mesh):
+    n_grp, n_seq = mesh.shape["grp"], mesh.shape["seq"]
+
+    def step(*args):
+        llm_grad, merger_pre, vit_out = args[0], args[4], args[5]
+        merger_out_w, merger_in_w, vit_fc2_w = args[8], args[9], args[10]
+        feat, (kb, hid), cw = llm_grad.shape[1], merger_out_w.shape, merger_in_w.shape[1]
+        vit, fw, rows = vit_out.shape[2], vit_fc2_w.shape[0], merger_pre.shape[0]
+        fits = (
+            n_grp == 2
+            and n_seq % 8 == 0
+            and feat % (2 * kb) == 0
+            and kb % 128 == 0
+            and hid % 256 == 0
+            and (2 * cw) % 128 == 0
+            and vit % (2 * cw) == 0
+            and vit % 256 == 0
+            and fw % 16 == 0
+            and rows == n_seq * SLOT
+            and rows % 16 == 0
+        )
+        if fits:
+            return fused_on_device(*args, n_grp=n_grp, n_seq=n_seq)
+        return on_device(*args)
+
     return jax.shard_map(
-        on_device,
+        step,
         mesh=mesh,
         in_specs=(
             P("seq", "grp"),

time: 298 us -> 141 us (0.47); the launches traced: 292 us -> 140 us
  Pallas kernels: 0 us -> 130 us
  waiting for transfers between devices: 120 us -> 0 us
  blocking collectives: 99.5 us -> 0 us
  matrix products: 15.2 us -> 0 us
  between operations: 14.3 us -> 0.64 us
  starting transfers between devices: 12.2 us -> 0 us
  other arithmetic: 11.3 us -> 0 us
  local copies, waits for them, and re-layouts: 19.6 us -> 8.78 us
    pallas_call x0 -> x1, Pallas kernels: none -> 130 us  [fused_on_device(): pl.pallas_call(functools.partial(fused_kernel, n_grp, n_seq), out_shape=(...]
    all_to_all x2 -> x0, waiting for transfers between devices: 79.6 us -> none  [the longest x1 60.7 us: on_device(): lax.all_to_all(weight_part.astype(jnp.bfloat16), 'seq', split_axis=0, con...]
    all_to_all x2 -> x0, blocking collectives: 74.8 us -> none  [the longest x1 49 us: on_device(): lax.all_to_all(folded.astype(jnp.bfloat16), 'seq', split_axis=0, concat_a...]
    all_gather x2 -> x0, waiting for transfers between devices: 39.4 us -> none  [the longest x1 39.4 us: on_device(): all_pre = lax.all_gather(pre_grad, 'seq', axis=0, tiled=True)]
    all_gather x2 -> x0, blocking collectives: 24.6 us -> none  [the longest x1 14 us: on_device(): lax.all_gather(part_rows, 'grp', axis=0).astype(jnp.float32)]
    dot_general x5 -> x0, matrix products: 15.2 us -> none  [the longest x1 3.86 us: on_device(): lax.dot_general(columns, activation, (((0,), (0,)), ((), ())), preferred_...]
    all_to_all x2 -> x0, starting transfers between devices: 12.1 us -> none  [the longest x1 6.46 us: on_device(): lax.all_to_all(weight_part.astype(jnp.bfloat16), 'seq', split_axis=0, con...]
    reshape x7 -> x1, local copies, waits for them, and re-layouts: 8.19 us -> 1.29 us  [fused_on_device(): ln_gain.reshape(1, vit)]
  transfers between devices with their start and end apart: 4 -> 0, of which waited for: 3 -> 0; matrix products, arithmetic and copies ran while one was open for 9% -> 0% of each run, Pallas kernels for 0% -> 0%
where the time goes in v1:
time: 141 us; the launch traced here: 140 us
  Pallas kernels  130 us (92%)
  local copies, waits for them, and re-layouts  8.78 us (6%)
    pallas_call x1, Pallas kernels, fused_on_device(): pl.pallas_call(functools.partial(fused_kernel, n_grp, n_seq), out_shape=(...  130 us
    unnamed x4, local copies, waits for them, and re-layouts  7.48 us

profile of v1, /device:TPU:27, one launch (start us, length us, event | category | flops | bytes accessed | tf_op | source)
XLA Modules:
  0.0 139.8 jit_solution(10017013146197823252)
XLA Ops:
  0.6 1.3 reshape.35.gain
  1.9 2.2 %copy.14.win = bf16[1280,320]{1,0:T(8,128)(2,1)} copy(bf16[1280,320]{0,1:T(8,128)(2,1)} %param.20) | data formatting | bytes 1638400 | tf_op args[9]
  4.1 130.4 %shard_map.130 = (bf16[96,1280]{1,0:T(8,128)(2,1)}, bf16[192,1280]{1,0:T(8,128)(2,1)}, f32[80,1280]{1,0:T(8,128)}) custom-call(bf16[256,4096]{1,0:T(8,128)(2,1)} %llm.1, s32[2,256]{1,0:T(2,128)} %bitcast.13, s32[1,256]{1,0:T(1,128)} %bitcast.14, s32[1,256]{1,0:T(1,128)} %bitcast.15, bf16[48,1280]{1,0:T(8,128)(2,1)} %bitcast.12, bf16[192,1280]{1,0:T(8,128)(2,1)} %bitcast.8, ...), custom_call_target="tpu_custom_call" | custom-call | tf_op jit(solution)/shard_map/pallas_call | solution.py:719
  134.6 1.7 %copy.18 = bf16[96,1,1280]{2,0,1:T(8,128)(2,1)} copy(bf16[96,1,1280]{2,0,1:T(8,128)(2,1)} %bitcast.11) | data formatting | bytes 491520
  136.2 1.8 %copy.19 = bf16[192,1,1280]{2,0,1:T(8,128)(2,1)} copy(bf16[192,1,1280]{2,0,1:T(8,128)(2,1)} %bitcast.10) | data formatting | bytes 983040
  138.1 1.8 %copy.20 = f32[80,1280]{1,0:T(8,128)} copy(f32[80,1280]{1,0:T(8,128)} %get-tuple-element.14) | data formatting | bytes 819200

commit v2 on v1

--- a/solution.py
+++ b/solution.py
@@ -182,18 +182,22 @@
     pg_out,
     fc1_out,
     wg_out,
+    grid_v,
+    owner_v,
+    start_v,
+    gain_v,
     llm_v,
     mpre_v,
     vout_v,
     vpre_v,
     wo,
-    wi2,
     wi,
     wf,
     act,
     fslope,
     gslope,
     rows_all,
+    relay,
     xin,
     xflat,
     xperm,
@@ -211,15 +215,12 @@
     mg,
     m4,
     pgall,
-    fc1_v,
     own3,
     y3s,
     ry3,
     z3s,
     rz3,
-    wg_v,
     ld_sem,
-    out_sem,
     send_sem,
     xw_sem,
     xag_sem,
@@ -233,7 +234,8 @@
     fz_sem,
     fy_sem,
     fc_sem,
-    pg_sem,
+    pgx_sem,
+    pgc_sem,
     ry3_sem,
     rz3_sem,
 ):
@@ -250,7 +252,7 @@
     tok, feat = llm.shape
     kc = 2 * wout.shape[0]
     hid = wout.shape[1]
-    cw = win.shape[1]
+    cw = win.shape[0]
     cc = 2 * cw
     vit = vout.shape[1]
     pslot = vout.shape[0]
@@ -260,6 +262,7 @@
     qg = feat // kc
     nt = 256
     fhalf = vit // 2
+    first_lanes = -(-fhalf // 256) * 128
 
     def dev(gg, zz, yy, c2):
         return (gg, (zz * 2 + yy) * 2 + c2)
@@ -267,6 +270,13 @@
     x_peer = dev(1 - g, z, y, c)
     y_peer = dev(g, z, 1 - y, c)
     c_peer = dev(g, z, y, 1 - c)
+
+    def zrel(d):
+        out = z
+        for k in range(nz.bit_length() - 1):
+            if d >> k & 1:
+                out = out + (1 << k) * (1 - 2 * (z // (1 << k) % 2))
+        return out
 
     sends = []
 
@@ -285,6 +295,29 @@
     def arrive(dst, rsem):
         pltpu.make_async_copy(dst, dst, rsem).wait()
 
+    def fc2_block(zz, yy, cc2):
+        return wf.at[dev(g, zz, yy, cc2)[1]]
+
+    def fc2_z(d):
+        own = wf.at[s]
+        remote(own, own, fz_sem.at[d], dev(g, zrel(d), y, c)).start()
+
+    def fc2_near():
+        own = wf.at[s]
+        remote(own, own, fy_sem.at[0], y_peer).start()
+        remote(own, own, fc_sem.at[0, 0], c_peer).start()
+
+    def fc2_y(d):
+        blk = fc2_block(zrel(d), y, c)
+        arrive(blk, fz_sem.at[d])
+        remote(blk, blk, fy_sem.at[d], y_peer).start()
+        remote(blk, blk, fc_sem.at[0, d], c_peer).start()
+
+    def fc2_core(d):
+        blk = fc2_block(zrel(d), 1 - y, c)
+        arrive(blk, fy_sem.at[d])
+        remote(blk, blk, fc_sem.at[1, d], c_peer).start()
+
     barrier = pltpu.get_barrier_semaphore()
 
     @pl.loop(0, n_grp * n_seq)
@@ -302,13 +335,19 @@
         cp.start()
         loads[name] = cp
 
+    load("grid", grid, grid_v)
+    load("owner", owner, owner_v)
+    load("start", start, start_v)
     for i in range(qg):
         load(("llm", i), llm.at[:, pl.ds(i * kc, kc)], llm_v.at[:, pl.ds(i * kc, kc)])
+    load("gain", gain, gain_v)
     load("vpre", vpre, vpre_v)
     load("mpre", mpre, mpre_v)
     wo_own = wo.at[pl.ds(pl.multiple_of(c * (kc // 2), 16), kc // 2)]
     load("wo", wout, wo_own)
-    load("wi", win, wi2.at[c])
+    wi_own = wi.at[pl.ds(pl.multiple_of(c * cw, 16), cw)]
+    wi_far = wi.at[pl.ds(pl.multiple_of((1 - c) * cw, 16), cw)]
+    load("wi", win, wi_own)
     load("wf", fc2, wf.at[s])
     load("vout", vout.at[pl.ds(pl.multiple_of(g * phalf, 16), phalf)], vout_v)
 
@@ -318,11 +357,13 @@
     o2 = small_div(rem, SLOT)
     slot = rem - o2 * SLOT
     img = iota((1, n_img), 1)
+    for name in ("grid", "owner", "start"):
+        loads[name].wait()
     shard_of = small_div(img, n_seq)
-    count = (grid[0:1, :] * grid[1:2, :]).astype(F32)
-    width = grid[1:2, :].astype(F32)
-    starts = start[...].astype(F32)
-    owners = owner[...]
+    count = (grid_v[0:1, :] * grid_v[1:2, :]).astype(F32)
+    width = grid_v[1:2, :].astype(F32)
+    starts = start_v[...].astype(F32)
+    owners = owner_v[...]
     mine = (owners == o2 * 2 + par) & (shard_of == s)
     first = sum_where(mine, jnp.broadcast_to(starts, mine.shape))
     many = sum_where(mine, jnp.broadcast_to(count, mine.shape))
@@ -333,52 +374,46 @@
         picked = jnp.dot(
             onehot, llm_v[:, i * kc : (i + 1) * kc], preferred_element_type=F32
         ).astype(BF16)
-        rows_all[g * qg + i, 0] = picked[:half]
-        rows_all[g * qg + i, 1] = picked[half:]
+        rows_all[i, 0] = picked[:half]
+        rows_all[i, 1] = picked[half:]
 
     pl.semaphore_wait(barrier, n_grp * n_seq - 1)
 
-    xag = []
     for i in range(qg):
-        blk = g * qg + i
-        cp = remote(rows_all.at[blk], rows_all.at[blk], xag_sem.at[i], x_peer)
-        cp.start()
-        xag.append(cp)
-
-    def is_self(qq, p):
-        return (qq == q) & (p == c)
-
-    selfs = []
-
-    def send_rows(qq, p):
-        src = rows_all.at[qq, p]
-        cp = remote(src, xin.at[s], xin_sem.at[s], (g, qq * 2 + p))
-        me = is_self(qq, p)
-        local = pltpu.make_async_copy(src, xin.at[s], xin_sem.at[s])
-
+        remote(rows_all.at[i, 1], relay.at[i], xag_sem.at[i], x_peer).start()
+
+    def unless(me, cp):
         @pl.when(jnp.logical_not(me))
         def _():
             cp.start()
 
+        sends.pop()
+        sends.append((cp, me))
+
+    def send_rows(src, qq, p):
+        cp = remote(src, xin.at[s], xin_sem.at[s], (g, qq * 2 + p))
+        me = (qq == q) & (p == c)
+
         @pl.when(me)
         def _():
-            local.start()
-
-        sends.pop()
-        sends.append((cp, me))
+            pltpu.make_async_copy(src, xin.at[s], xin_sem.at[s]).start()
+
+        unless(me, cp)
 
     for i in range(qg):
-        for p in range(2):
-            send_rows(g * qg + i, p)
-
+        send_rows(rows_all.at[i, 0], g * qg + i, 0)
+
+    loads["wf"].wait()
     remote(wout, wo_own, xw_sem.at[0], c_peer).start()
-    remote(win, wi2.at[c], xw_sem.at[1], c_peer).start()
+    remote(win, wi_own, xw_sem.at[1], c_peer).start()
 
     for i in range(qg):
-        arrive(rows_all.at[(1 - g) * qg + i], xag_sem.at[i])
-        for p in range(2):
-            send_rows((1 - g) * qg + i, p)
-
+        arrive(relay.at[i], xag_sem.at[i])
+        send_rows(relay.at[i], (1 - g) * qg + i, 1)
+
+    fc2_z(1)
+    fc2_z(3)
+    fc2_near()
     loads["vpre"].wait()
     tile = 64 if pslot % 64 == 0 else 16
 
@@ -405,14 +440,21 @@
     perm = (iota((half * n_seq, half * n_seq), 1) == want).astype(BF16)
 
     loads["wi"].wait()
-    arrive(wi2.at[1 - c], xw_sem.at[1])
-    wi[...] = jnp.concatenate([wi2[0], wi2[1]], axis=1)
+    arrive(wi_far, xw_sem.at[1])
     loads["wo"].wait()
     arrive(wo.at[pl.ds(pl.multiple_of((1 - c) * (kc // 2), 16), kc // 2)], xw_sem.at[0])
 
-    for src in range(n_seq):
-        arrive(xin.at[src], xin_sem.at[src])
-        xflat[src * half : (src + 1) * half, :] = xin[src].astype(F32)
+    first_hand = (g + c + q // qg) % 2 == 0
+    for d in range(nz):
+        for k in range(4):
+            src = zrel(d) * 4 + k
+            arrive(xin.at[src], xin_sem.at[src])
+            unless(
+                jnp.logical_not(first_hand),
+                remote(xin.at[src], xin.at[src], xin_sem.at[src], x_peer),
+            )
+            at = pl.ds(pl.multiple_of(src * half, 8), half)
+            xflat[at, :] = xin[src].astype(F32)
 
     @pl.loop(0, kc // nt)
     def _(t):
@@ -434,13 +476,13 @@
                 out[zz, :, sl] = got[zz * rows : (zz + 1) * rows].astype(out.dtype)
 
     part1(1 - y, ys)
-    order = [d for d in range(1, nz)] + [0]
+    order = list(range(nz - 1, -1, -1))
     for d in order:
-        zz = (z + d) % nz
+        zz = zrel(d)
         remote(ys.at[zz], ry.at[zz], ry_sem.at[d], y_peer).start()
     part1(y, own1)
     for d in order:
-        zz = (z + d) % nz
+        zz = zrel(d)
         arrive(ry.at[zz], ry_sem.at[d])
         total = own1[zz] + ry[zz].astype(F32)
         if d:
@@ -448,26 +490,33 @@
             remote(zs.at[d], rz.at[d], rz_sem.at[d], dev(g, zz, y, c)).start()
         else:
             unit = total
-    for d in range(1, nz):
+    for d in order[:-1]:
         arrive(rz.at[d], rz_sem.at[d])
         unit = unit + rz[d].astype(F32)
     pre = (gslope[...] * unit.astype(BF16).astype(F32)).astype(BF16)
     allp[q] = pre
 
     remote(allp.at[q], allp.at[q], agy_sem.at[0], y_peer).start()
-    for d in range(1, nz):
-        remote(allp.at[q], allp.at[q], agz_sem.at[d], dev(g, (z + d) % nz, y, c)).start()
-    for d in range(1, nz):
-        qq = ((z + nz - d) % nz) * 2 + y
+    for d in order[:-1]:
+        remote(allp.at[q], allp.at[q], agz_sem.at[d], dev(g, zrel(d), y, c)).start()
+    near_first = [0] + order[:-1]
+    for d in near_first[1:]:
+        qq = zrel(d) * 2 + y
         arrive(allp.at[qq], agz_sem.at[d])
         remote(allp.at[qq], allp.at[qq], agy_sem.at[d], y_peer).start()
 
-    for d in range(nz):
-        zz = (z + nz - d) % nz
+    fc2_z(2)
+    fc2_y(1)
+    fc2_y(3)
+    for d in near_first:
+        zz = zrel(d)
         arrive(allp.at[zz * 2 + 1 - y], agy_sem.at[d])
         for yo in range(2):
-            p2[yo * rows : (yo + 1) * rows, :] = jnp.dot(
-                allp[zz * 2 + yo], wi[...], preferred_element_type=F32
+            p2[yo * rows : (yo + 1) * rows, :] = lax.dot_general(
+                allp[zz * 2 + yo],
+                wi[...],
+                (((1,), (1,)), ((), ())),
+                preferred_element_type=F32,
             )
         for e in range(2):
             yo = y + e - 2 * y * e
@@ -477,14 +526,8 @@
             own2[d, e] = p2[near, :].astype(BF16)
         remote(xs.at[d], rx.at[d], rx_sem.at[d], x_peer).start()
 
-    loads["wf"].wait()
-    for d in range(1, nz):
-        remote(wf.at[s], wf.at[s], fz_sem.at[d], dev(g, (z + d) % nz, y, c)).start()
-    remote(wf.at[s], wf.at[s], fy_sem.at[0], y_peer).start()
-    remote(wf.at[s], wf.at[s], fc_sem.at[0, 0], c_peer).start()
-
-    for d in range(nz):
-        zz = (z + nz - d) % nz
+    for d in near_first:
+        zz = zrel(d)
         arrive(rx.at[d], rx_sem.at[d])
         for e in range(2):
             yo = y + e - 2 * y * e
@@ -494,12 +537,6 @@
             else:
                 a2s[d, e] = total
                 remote(a2s.at[d, e], mg.at[q], mg_sem.at[q], dev(g, zz, yo, c)).start()
-
-    for d in range(1, nz):
-        blk = wf.at[dev(g, (z + nz - d) % nz, y, c)[1]]
-        arrive(blk, fz_sem.at[d])
-        remote(blk, blk, fy_sem.at[d], y_peer).start()
-        remote(blk, blk, fc_sem.at[0, d], c_peer).start()
 
     shape = (phalf, phalf)
     r = iota((phalf, 1), 0)
@@ -521,6 +558,7 @@
     target = (2 * row_in + upper) * (2 * wide) + 2 * col_in + (comp - 2 * upper)
     table = ((src_c == src_r) & (slot < many) & (target == place)).astype(BF16)
     loads["vout"].wait()
+    loads["gain"].wait()
 
     per = vit // cc
     for qq in range(nq):
@@ -531,67 +569,91 @@
 
         part, piece = qq // per, qq % per
         m4[part * half : (part + 1) * half, piece * cc : (piece + 1) * cc] = mg[qq].astype(F32)
+    fc2_y(2)
+    scales = jnp.concatenate([gain_v[k : k + 1, :] for k in range(vit // 128)], axis=1)
     patch_in = jnp.dot(table, m4[...].astype(BF16), preferred_element_type=F32)
-    pg = norm_backward(patch_in, vout_v[...].astype(F32), gain[...]).astype(BF16)
-    own_rows = pgall.at[c, g]
+    pg = norm_backward(patch_in, vout_v[...].astype(F32), scales).astype(BF16)
     pgall[c, g] = pg
-    remote(own_rows, own_rows, pg_sem.at[0], x_peer).start()
-    remote(own_rows, own_rows, pg_sem.at[1], c_peer).start()
-    put_pg = pltpu.make_async_copy(own_rows, pg_out, out_sem.at[0])
-    put_pg.start()
-
-    for d in range(nz):
-        blk = wf.at[dev(g, (z + nz - d) % nz, 1 - y, c)[1]]
-        arrive(blk, fy_sem.at[d])
-        remote(blk, blk, fc_sem.at[1, d], c_peer).start()
-
-    far_rows = pgall.at[c, 1 - g]
-    arrive(far_rows, pg_sem.at[0])
-    remote(far_rows, far_rows, pg_sem.at[2], c_peer).start()
+    pg_out[...] = pg
+    zh = nz // 2
+    cuts = [(0, first_lanes), (first_lanes, fhalf - first_lanes)]
+
+    def piece(i, j, side, k):
+        lane = pl.multiple_of(side * fhalf + cuts[k][0], 128)
+        return pgall.at[i, j, :, pl.ds(lane, cuts[k][1])]
+
+    for k in range(2):
+        for side in (1 - c, c):
+            at = piece(c, g, side, k)
+            is_far = 0 if side is c else 1
+            remote(at, at, pgx_sem.at[k, is_far], x_peer).start()
+        at = piece(c, g, 1 - c, k)
+        remote(at, at, pgc_sem.at[k, 0], c_peer).start()
+    fc2_core(0)
+    fc2_core(1)
+    fc2_core(3)
     arrive(act.at[1 - c], xw_sem.at[2])
-    arrive(pgall.at[1 - c, g], pg_sem.at[1])
-    arrive(pgall.at[1 - c, 1 - g], pg_sem.at[2])
-
-    lane = pl.multiple_of(c * fhalf, 128)
     quarter = 2 * fw
-    zh = nz // 2
-    lhs = [
-        pgall[i, j, :, pl.ds(lane, fhalf)].T for i in range(2) for j in range(2)
-    ]
-    lhs = jnp.concatenate(lhs, axis=1)
-    own3[...] = jnp.dot(
-        lhs, jnp.concatenate([act[0], act[1]], axis=0), preferred_element_type=F32
-    )
-    for zz in range(zh):
-        base = pl.multiple_of((zz * 2 + 1 - y) * quarter, 16)
-        for c2 in range(2):
-            y3s[zz, c2] = own3[pl.ds(base + c2 * fw, fw), :].astype(BF16)
-            remote(y3s.at[zz, c2], ry3.at[zz, c2], ry3_sem.at[zz, c2], y_peer).start()
+    acts = act.reshape(2 * pslot, hid)
+    hh = hid // 2
+    sent = 0
+    for k in range(2):
+        at = piece(c, 1 - g, 1 - c, k)
+        arrive(at, pgx_sem.at[k, 1])
+        remote(at, at, pgc_sem.at[k, 1], c_peer).start()
+        arrive(piece(c, 1 - g, c, k), pgx_sem.at[k, 0])
+        arrive(piece(1 - c, g, c, k), pgc_sem.at[k, 0])
+        arrive(piece(1 - c, 1 - g, c, k), pgc_sem.at[k, 1])
+        begin, size = cuts[k]
+        lhs = jnp.concatenate(
+            [piece(i, j, c, k)[...] for i in range(2) for j in range(2)], axis=0
+        )
+        ready = zh if k else (begin + size) // (2 * quarter)
+        for hf in range(2):
+            col = slice(hf * hh, (hf + 1) * hh)
+            own3[begin : begin + size, col] = lax.dot_general(
+                lhs, acts[:, col], (((0,), (0,)), ((), ())), preferred_element_type=F32
+            )
+            for zz in range(sent, ready):
+                base = pl.multiple_of((zz * 2 + 1 - y) * quarter, 16)
+                for c2 in range(2):
+                    kk = zz * 2 + c2
+                    y3s[hf, kk] = own3[pl.ds(base + c2 * fw, fw), col].astype(BF16)
+                    remote(
+                        y3s.at[hf, kk], ry3.at[hf, kk], ry3_sem.at[hf, kk], y_peer
+                    ).start()
+        sent = ready
     for zz in range(zh):
         base = pl.multiple_of((zz * 2 + y) * quarter, 16)
-        for c2 in range(2):
-            arrive(ry3.at[zz, c2], ry3_sem.at[zz, c2])
-            total = own3[pl.ds(base + c2 * fw, fw), :] + ry3[zz, c2].astype(F32)
-            to_z = c * zh + zz
-            me = (to_z == z) & (c2 == c)
-            z3s[zz, c2] = total.astype(BF16)
-            cp = remote(z3s.at[zz, c2], rz3.at[z], rz3_sem.at[z], dev(g, to_z, y, c2))
-
-            @pl.when(me)
-            def _():
-                rz3[z] = total.astype(BF16)
-
-            @pl.when(jnp.logical_not(me))
-            def _():
-                cp.start()
-
-            sends.pop()
-            sends.append((cp, me))
-
+        for hf in range(2):
+            col = slice(hf * hh, (hf + 1) * hh)
+            for c2 in range(2):
+                k = zz * 2 + c2
+                arrive(ry3.at[hf, k], ry3_sem.at[hf, k])
+                total = own3[pl.ds(base + c2 * fw, fw), col] + ry3[hf, k].astype(F32)
+                to_z = c * zh + zz
+                me = (to_z == z) & (c2 == c)
+                z3s[hf, k] = total.astype(BF16)
+
+                @pl.when(me)
+                def _():
+                    rz3[z, hf] = total.astype(BF16)
+
+                unless(
+                    me,
+                    remote(
+                        z3s.at[hf, k],
+                        rz3.at[z, hf],
+                        rz3_sem.at[z, hf],
+                        dev(g, to_z, y, c2),
+                    ),
+                )
+
+    fc2_core(2)
     for d in range(nz):
         for e in range(2):
             yy = y + e - 2 * y * e
-            arrive(wf.at[dev(g, (z + nz - d) % nz, yy, 1 - c)[1]], fc_sem.at[e, d])
+            arrive(fc2_block(zrel(d), yy, 1 - c), fc_sem.at[e, d])
     own_pg = jnp.concatenate([pgall[c, 0], pgall[c, 1]], axis=0)
     wfull = wf.reshape(vit, hid)
 
@@ -599,22 +661,18 @@
     def _(t):
         sl = pl.ds(pl.multiple_of(t * nt, nt), nt)
         got = jnp.dot(own_pg, wfull[:, sl], preferred_element_type=F32)
-        fc1_v[:, sl] = (fslope[:, sl] * got).astype(BF16)
-
-    put_fc1 = pltpu.make_async_copy(fc1_v, fc1_out, out_sem.at[1])
-    put_fc1.start()
-
-    total = jnp.zeros((fw, hid), F32)
-    for zz in range(nz):
-
-        @pl.when(jnp.logical_not((zz == z) & (c == z // zh)))
-        def _():
-            arrive(rz3.at[zz], rz3_sem.at[zz])
-
-        total = total + rz3[zz].astype(F32)
-    wg_v[...] = total
-    put_wg = pltpu.make_async_copy(wg_v, wg_out, out_sem.at[2])
-    put_wg.start()
+        fc1_out[:, sl] = (fslope[:, sl] * got).astype(BF16)
+
+    for hf in range(2):
+        total = jnp.zeros((fw, hh), F32)
+        for zz in range(nz):
+
+            @pl.when(jnp.logical_not((zz == z) & (c == z // zh)))
+            def _():
+                arrive(rz3.at[zz, hf], rz3_sem.at[zz, hf])
+
+            total = total + rz3[zz, hf].astype(F32)
+        wg_out[:, hf * hh : (hf + 1) * hh] = total
 
     for item in sends:
         if isinstance(item, tuple):
@@ -626,9 +684,10 @@
 
         else:
             item.wait_send()
-    put_pg.wait()
-    put_fc1.wait()
-    put_wg.wait()
+
+
+def in_hbm(x):
+    return pltpu.with_memory_space_constraint(x, pltpu.HBM)
 
 
 def fused_on_device(
@@ -657,22 +716,26 @@
     half, phalf = rows // 2, pslot // 2
     nz, nq, kc, cc = n_seq // 4, n_seq // 2, 2 * kb, 2 * cw
     qg = feat // kc
-    vmem, anyspace = pltpu.VMEM, pl.BlockSpec(memory_space=pl.ANY)
+    vmem, anyspace = pltpu.VMEM, pl.BlockSpec(memory_space=pltpu.HBM)
     vspec = pl.BlockSpec(memory_space=pltpu.VMEM)
     dma = pltpu.SemaphoreType.DMA
     scratch = [
+        vmem((2, n_img), jnp.int32),
+        vmem((1, n_img), jnp.int32),
+        vmem((1, n_img), jnp.int32),
+        vmem((vit // 128, 128), F32),
         vmem((tok, feat), BF16),
         vmem((rows, hid), BF16),
         vmem((phalf, vit), BF16),
         vmem((pslot, hid), BF16),
         vmem((kc, hid), BF16),
-        vmem((2, hid, cw), BF16),
-        vmem((hid, cc), BF16),
+        vmem((cc, hid), BF16),
         vmem((n_seq, fw, hid), BF16),
         vmem((2, pslot, hid), BF16),
         vmem((pslot, hid), F32),
         vmem((rows, hid), F32),
-        vmem((nq, 2, half, kc), BF16),
+        vmem((qg, 2, half, kc), BF16),
+        vmem((qg, half, kc), BF16),
         vmem((n_seq, half, kc), BF16),
         vmem((n_seq * half, kc), F32),
         vmem((n_seq * half, kc), BF16),
@@ -690,15 +753,12 @@
         vmem((nq, half, cc), BF16),
         vmem((phalf, vit), F32),
         vmem((2, 2, phalf, vit), BF16),
-        vmem((pslot, hid), BF16),
         vmem((vit // 2, hid), F32),
-        vmem((nz // 2, 2, fw, hid), BF16),
-        vmem((nz // 2, 2, fw, hid), BF16),
-        vmem((nz // 2, 2, fw, hid), BF16),
-        vmem((nz, fw, hid), BF16),
-        vmem((fw, hid), F32),
-        dma((qg + 6,)),
-        dma((3,)),
+        vmem((2, nz, fw, hid // 2), BF16),
+        vmem((2, nz, fw, hid // 2), BF16),
+        vmem((2, nz, fw, hid // 2), BF16),
+        vmem((nz, 2, fw, hid // 2), BF16),
+        dma((qg + 10,)),
         dma((256,)),
         dma((3,)),
         dma((qg,)),
@@ -712,9 +772,10 @@
         dma((nz,)),
         dma((nz,)),
         dma((2, nz)),
-        dma((3,)),
-        dma((nz // 2, 2)),
-        dma((nz,)),
+        dma((2, 2)),
+        dma((2, 2)),
+        dma((2, nz)),
+        dma((nz, 2)),
     ]
     pg, fc1, wg = pl.pallas_call(
         functools.partial(fused_kernel, n_grp, n_seq),
@@ -723,36 +784,24 @@
             jax.ShapeDtypeStruct((pslot, hid), BF16),
             jax.ShapeDtypeStruct((fw, hid), F32),
         ),
-        in_specs=[
-            anyspace,
-            vspec,
-            vspec,
-            vspec,
-            anyspace,
-            anyspace,
-            anyspace,
-            vspec,
-            anyspace,
-            anyspace,
-            anyspace,
-        ],
-        out_specs=(anyspace, anyspace, anyspace),
+        in_specs=[anyspace] * 11,
+        out_specs=(vspec, vspec, vspec),
         scratch_shapes=scratch,
         compiler_params=pltpu.CompilerParams(
-            collective_id=0, has_side_effects=True, vmem_limit_bytes=60 * 1024 * 1024
+            collective_id=0, has_side_effects=True, vmem_limit_bytes=40 * 1024 * 1024
         ),
     )(
-        llm_grad,
-        image_grid.T,
-        image_owner.reshape(1, n_img),
-        row_start.reshape(1, n_img),
-        merger_pre.reshape(rows, hid),
-        vit_out.reshape(pslot, vit),
-        vit_pre.reshape(pslot, hid),
-        ln_gain.reshape(1, vit),
-        merger_out_w,
-        merger_in_w,
-        vit_fc2_w,
+        in_hbm(llm_grad),
+        in_hbm(image_grid.T),
+        in_hbm(image_owner.reshape(1, n_img)),
+        in_hbm(row_start.reshape(1, n_img)),
+        in_hbm(merger_pre.reshape(rows, hid)),
+        in_hbm(vit_out.reshape(pslot, vit)),
+        in_hbm(vit_pre.reshape(pslot, hid)),
+        in_hbm(ln_gain.reshape(vit // 128, 128)),
+        in_hbm(merger_out_w),
+        in_hbm(merger_in_w.T),
+        in_hbm(vit_fc2_w),
     )
     return pg.reshape(phalf, 1, vit), fc1.reshape(pslot, 1, hid), wg
 
@@ -767,7 +816,8 @@
         vit, fw, rows = vit_out.shape[2], vit_fc2_w.shape[0], merger_pre.shape[0]
         fits = (
             n_grp == 2
-            and n_seq % 8 == 0
+            and n_seq >= 8
+            and n_seq & (n_seq - 1) == 0
             and feat % (2 * kb) == 0
             and kb % 128 == 0
             and hid % 256 == 0

time: 141 us -> 106 us (0.75)
  Pallas kernels: 130 us -> 103 us
  local copies, waits for them, and re-layouts: 8.78 us -> 2.22 us
    pallas_call x1, Pallas kernels: 130 us -> 103 us  [fused_on_device(): pl.pallas_call(functools.partial(fused_kernel, n_grp, n_seq), out_shape=(...]
    unnamed x4 -> x3, local copies, waits for them, and re-layouts: 7.48 us -> 2.22 us
where the time goes in v2:
time: 106 us
  Pallas kernels  103 us (97%)
  local copies, waits for them, and re-layouts  2.22 us (2%)
    pallas_call x1, Pallas kernels, fused_on_device(): pl.pallas_call(functools.partial(fused_kernel, n_grp, n_seq), out_shape=(...  103 us
    unnamed x3, local copies, waits for them, and re-layouts  2.22 us

profile of v2, /device:TPU:27, one launch (start us, length us, event | category | flops | bytes accessed | tf_op | source)
XLA Modules:
  0.0 106.0 jit_solution(17706684475700165040)
XLA Ops:
  0.6 103.1 %shard_map.130 = (bf16[96,1280]{1,0:T(8,128)(2,1)S(1)}, bf16[192,1280]{1,0:T(8,128)(2,1)S(1)}, f32[80,1280]{1,0:T(8,128)S(1)}) custom-call(bf16[256,4096]{1,0:T(8,128)(2,1)} %llm.1, s32[2,256]{1,0:T(2,128)} %bitcast.17, s32[1,256]{1,0:T(1,128)} %bitcast.18, s32[1,256]{1,0:T(1,128)} %bitcast.19, bf16[48,1280]{1,0:T(8,128)(2,1)} %bitcast.15, ...), custom_call_target="tpu_custom_call" | custom-call | tf_op jit(solution)/shard_map/pallas_call | solution.py:780
  103.8 0.7 copy.17
  104.5 0.8 copy.18
  105.3 0.8 copy.19

commit v3 on v2

--- a/solution.py
+++ b/solution.py
@@ -234,7 +234,7 @@
     fz_sem,
     fy_sem,
     fc_sem,
-    pgx_sem,
+    mgx_sem,
     pgc_sem,
     ry3_sem,
     rz3_sem,
@@ -349,7 +349,7 @@
     wi_far = wi.at[pl.ds(pl.multiple_of((1 - c) * cw, 16), cw)]
     load("wi", win, wi_own)
     load("wf", fc2, wf.at[s])
-    load("vout", vout.at[pl.ds(pl.multiple_of(g * phalf, 16), phalf)], vout_v)
+    load("vout", vout, vout_v)
 
     r = iota((rows, 1), 0)
     par = small_div(r, half)
@@ -439,6 +439,7 @@
     want = src_s * half + (zo * 2 + yo) * SLOT + slot
     perm = (iota((half * n_seq, half * n_seq), 1) == want).astype(BF16)
 
+    loads["gain"].wait()
     loads["wi"].wait()
     arrive(wi_far, xw_sem.at[1])
     loads["wo"].wait()
@@ -465,59 +466,74 @@
 
     hrows = nz * rows
 
-    def part1(yy, out):
+    hh = hid // 2
+    order = list(range(nz - 1, -1, -1))
+
+    def part1(yy, hf, out):
         lhs = xperm[pl.ds(pl.multiple_of(yy * hrows, 16), hrows), :]
-
-        @pl.loop(0, hid // nt)
-        def _(t):
-            sl = pl.ds(pl.multiple_of(t * nt, nt), nt)
-            got = jnp.dot(lhs, wo[:, sl], preferred_element_type=F32)
-            for zz in range(nz):
-                out[zz, :, sl] = got[zz * rows : (zz + 1) * rows].astype(out.dtype)
-
-    part1(1 - y, ys)
-    order = list(range(nz - 1, -1, -1))
+        got = jnp.dot(lhs, wo[:, hf * hh : (hf + 1) * hh], preferred_element_type=F32)
+        for zz in range(nz):
+            out[hf, zz] = got[zz * rows : (zz + 1) * rows].astype(out.dtype)
+
+    for hf in range(2):
+        part1(1 - y, hf, ys)
+        for d in order:
+            zz = zrel(d)
+            remote(ys.at[hf, zz], ry.at[hf, zz], ry_sem.at[hf, d], y_peer).start()
+    for hf in range(2):
+        part1(y, hf, own1)
+    units = {}
+
+    def over_y(hf, d):
+        zz = zrel(d)
+        arrive(ry.at[hf, zz], ry_sem.at[hf, d])
+        total = own1[hf, zz] + ry[hf, zz].astype(F32)
+        if d:
+            zs[hf, d] = total.astype(BF16)
+            remote(zs.at[hf, d], rz.at[hf, d], rz_sem.at[hf, d], dev(g, zz, y, c)).start()
+        else:
+            units[hf] = total
+
+    def over_z(hf):
+        unit = units[hf]
+        for d in order[:-1]:
+            arrive(rz.at[hf, d], rz_sem.at[hf, d])
+            unit = unit + rz[hf, d].astype(F32)
+        slope = gslope[:, hf * hh : (hf + 1) * hh]
+        allp[hf, q] = (slope * unit.astype(BF16).astype(F32)).astype(BF16)
+        mine = allp.at[hf, q]
+        remote(mine, mine, agy_sem.at[hf, 0], y_peer).start()
+        for d in order[:-1]:
+            remote(mine, mine, agz_sem.at[hf, d], dev(g, zrel(d), y, c)).start()
+
     for d in order:
+        over_y(0, d)
+    for d in order:
+        over_y(1, d)
+    over_z(0)
+    over_z(1)
+    fc2_y(1)
+    near_first = [0] + order[:-1]
+    for hf in range(2):
+        for d in near_first[1:]:
+            qq = zrel(d) * 2 + y
+            arrive(allp.at[hf, qq], agz_sem.at[hf, d])
+            remote(allp.at[hf, qq], allp.at[hf, qq], agy_sem.at[hf, d], y_peer).start()
+
+    fc2_z(2)
+    fc2_y(3)
+    def columns_of(d):
         zz = zrel(d)
-        remote(ys.at[zz], ry.at[zz], ry_sem.at[d], y_peer).start()
-    part1(y, own1)
-    for d in order:
-        zz = zrel(d)
-        arrive(ry.at[zz], ry_sem.at[d])
-        total = own1[zz] + ry[zz].astype(F32)
-        if d:
-            zs[d] = total.astype(BF16)
-            remote(zs.at[d], rz.at[d], rz_sem.at[d], dev(g, zz, y, c)).start()
-        else:
-            unit = total
-    for d in order[:-1]:
-        arrive(rz.at[d], rz_sem.at[d])
-        unit = unit + rz[d].astype(F32)
-    pre = (gslope[...] * unit.astype(BF16).astype(F32)).astype(BF16)
-    allp[q] = pre
-
-    remote(allp.at[q], allp.at[q], agy_sem.at[0], y_peer).start()
-    for d in order[:-1]:
-        remote(allp.at[q], allp.at[q], agz_sem.at[d], dev(g, zrel(d), y, c)).start()
-    near_first = [0] + order[:-1]
-    for d in near_first[1:]:
-        qq = zrel(d) * 2 + y
-        arrive(allp.at[qq], agz_sem.at[d])
-        remote(allp.at[qq], allp.at[qq], agy_sem.at[d], y_peer).start()
-
-    fc2_z(2)
-    fc2_y(1)
-    fc2_y(3)
-    for d in near_first:
-        zz = zrel(d)
-        arrive(allp.at[zz * 2 + 1 - y], agy_sem.at[d])
-        for yo in range(2):
-            p2[yo * rows : (yo + 1) * rows, :] = lax.dot_general(
-                allp[zz * 2 + yo],
-                wi[...],
+        got = jnp.zeros((2 * rows, cc), F32)
+        for hf in range(2):
+            arrive(allp.at[hf, zz * 2 + 1 - y], agy_sem.at[hf, d])
+            got = got + lax.dot_general(
+                allp[hf, pl.ds(zz * 2, 2)].reshape(2 * rows, hh),
+                wi[:, hf * hh : (hf + 1) * hh],
                 (((1,), (1,)), ((), ())),
                 preferred_element_type=F32,
             )
+        p2[...] = got
         for e in range(2):
             yo = y + e - 2 * y * e
             far = pl.ds(pl.multiple_of(yo * rows + (1 - g) * half, 8), half)
@@ -526,55 +542,70 @@
             own2[d, e] = p2[near, :].astype(BF16)
         remote(xs.at[d], rx.at[d], rx_sem.at[d], x_peer).start()
 
-    for d in near_first:
-        zz = zrel(d)
+    def to_owners(d):
         arrive(rx.at[d], rx_sem.at[d])
-        for e in range(2):
+        for e in (1, 0):
             yo = y + e - 2 * y * e
             total = (own2[d, e].astype(F32) + rx[d, e].astype(F32)).astype(BF16)
             if d == 0 and e == 0:
-                mg[q] = total
+                mg[g, q] = total
+                remote(mg.at[g, q], mg.at[g, q], mgx_sem.at[q], x_peer).start()
             else:
                 a2s[d, e] = total
-                remote(a2s.at[d, e], mg.at[q], mg_sem.at[q], dev(g, zz, yo, c)).start()
-
-    shape = (phalf, phalf)
-    r = iota((phalf, 1), 0)
-    src_r = small_div(r, 4 * SLOT)
-    place = r - src_r * (4 * SLOT)
-    mine = (owners == s) & (shard_of == src_r + g * (n_seq // 2))
-    many = sum_where(mine, jnp.broadcast_to(count, mine.shape))
-    wide = sum_where(mine, jnp.broadcast_to(width, mine.shape))
-    col = iota(shape, 1)
-    comp = small_div(col, half)
-    rem = col - comp * half
-    src_c = small_div(rem, SLOT)
-    slot = rem - src_c * SLOT
-    row_in = jnp.zeros(shape, jnp.int32)
-    for k in range(1, SLOT):
-        row_in = row_in + (slot >= k * wide).astype(jnp.int32)
-    col_in = slot - row_in * wide
-    upper = comp >> 1
-    target = (2 * row_in + upper) * (2 * wide) + 2 * col_in + (comp - 2 * upper)
-    table = ((src_c == src_r) & (slot < many) & (target == place)).astype(BF16)
+                remote(
+                    a2s.at[d, e], mg.at[g, q], mg_sem.at[q], dev(g, zrel(d), yo, c)
+                ).start()
+
+    for k, d in enumerate(near_first):
+        columns_of(d)
+        if k:
+            to_owners(near_first[k - 1])
+    to_owners(near_first[-1])
+    def slot_table(gg):
+        shape = (phalf, phalf)
+        r = iota((phalf, 1), 0)
+        src_r = small_div(r, 4 * SLOT)
+        place = r - src_r * (4 * SLOT)
+        mine = (owners == s) & (shard_of == src_r + gg * (n_seq // 2))
+        many = sum_where(mine, jnp.broadcast_to(count, mine.shape))
+        wide = sum_where(mine, jnp.broadcast_to(width, mine.shape))
+        col = iota(shape, 1)
+        comp = small_div(col, half)
+        rem = col - comp * half
+        src_c = small_div(rem, SLOT)
+        slot = rem - src_c * SLOT
+        row_in = jnp.zeros(shape, jnp.int32)
+        for k in range(1, SLOT):
+            row_in = row_in + (slot >= k * wide).astype(jnp.int32)
+        col_in = slot - row_in * wide
+        upper = comp >> 1
+        target = (2 * row_in + upper) * (2 * wide) + 2 * col_in + (comp - 2 * upper)
+        return ((src_c == src_r) & (slot < many) & (target == place)).astype(BF16)
+
+    per = vit // cc
+    scales = jnp.concatenate([gain_v[k : k + 1, :] for k in range(vit // 128)], axis=1)
+
+    def norm_half(gg, table):
+        for qq in range(nq):
+            part, spot = qq // per, qq % per
+            m4[part * half : (part + 1) * half, spot * cc : (spot + 1) * cc] = mg[
+                gg, qq
+            ].astype(F32)
+        patch_in = jnp.dot(table, m4[...].astype(BF16), preferred_element_type=F32)
+        saved = vout_v[pl.ds(pl.multiple_of(gg * phalf, 16), phalf), :].astype(F32)
+        pg = norm_backward(patch_in, saved, scales).astype(BF16)
+        pgall[c, gg] = pg
+        return pg
+
     loads["vout"].wait()
-    loads["gain"].wait()
-
-    per = vit // cc
-    for qq in range(nq):
-
-        @pl.when(qq != q)
-        def _():
-            arrive(mg.at[qq], mg_sem.at[qq])
-
-        part, piece = qq // per, qq % per
-        m4[part * half : (part + 1) * half, piece * cc : (piece + 1) * cc] = mg[qq].astype(F32)
+    far_g = 1 - g
+    near_table, far_table = slot_table(g), slot_table(far_g)
+    for d in near_first:
+        for e in (1, 0) if d else (1,):
+            qq = zrel(d) * 2 + y + e - 2 * y * e
+            arrive(mg.at[g, qq], mg_sem.at[qq])
+            remote(mg.at[g, qq], mg.at[g, qq], mgx_sem.at[qq], x_peer).start()
     fc2_y(2)
-    scales = jnp.concatenate([gain_v[k : k + 1, :] for k in range(vit // 128)], axis=1)
-    patch_in = jnp.dot(table, m4[...].astype(BF16), preferred_element_type=F32)
-    pg = norm_backward(patch_in, vout_v[...].astype(F32), scales).astype(BF16)
-    pgall[c, g] = pg
-    pg_out[...] = pg
     zh = nz // 2
     cuts = [(0, first_lanes), (first_lanes, fhalf - first_lanes)]
 
@@ -582,26 +613,26 @@
         lane = pl.multiple_of(side * fhalf + cuts[k][0], 128)
         return pgall.at[i, j, :, pl.ds(lane, cuts[k][1])]
 
+    def to_core(j, k, which):
+        at = piece(c, j, 1 - c, k)
+        remote(at, at, pgc_sem.at[k, which], c_peer).start()
+
+    pg_out[...] = norm_half(g, near_table)
     for k in range(2):
-        for side in (1 - c, c):
-            at = piece(c, g, side, k)
-            is_far = 0 if side is c else 1
-            remote(at, at, pgx_sem.at[k, is_far], x_peer).start()
-        at = piece(c, g, 1 - c, k)
-        remote(at, at, pgc_sem.at[k, 0], c_peer).start()
+        to_core(g, k, 0)
+    for qq in range(nq):
+        arrive(mg.at[far_g, qq], mgx_sem.at[qq])
+    norm_half(far_g, far_table)
+    for k in range(2):
+        to_core(far_g, k, 1)
     fc2_core(0)
     fc2_core(1)
     fc2_core(3)
     arrive(act.at[1 - c], xw_sem.at[2])
     quarter = 2 * fw
     acts = act.reshape(2 * pslot, hid)
-    hh = hid // 2
     sent = 0
     for k in range(2):
-        at = piece(c, 1 - g, 1 - c, k)
-        arrive(at, pgx_sem.at[k, 1])
-        remote(at, at, pgc_sem.at[k, 1], c_peer).start()
-        arrive(piece(c, 1 - g, c, k), pgx_sem.at[k, 0])
         arrive(piece(1 - c, g, c, k), pgc_sem.at[k, 0])
         arrive(piece(1 - c, 1 - g, c, k), pgc_sem.at[k, 1])
         begin, size = cuts[k]
@@ -726,7 +757,7 @@
         vmem((vit // 128, 128), F32),
         vmem((tok, feat), BF16),
         vmem((rows, hid), BF16),
-        vmem((phalf, vit), BF16),
+        vmem((pslot, vit), BF16),
         vmem((pslot, hid), BF16),
         vmem((kc, hid), BF16),
         vmem((cc, hid), BF16),
@@ -739,18 +770,18 @@
         vmem((n_seq, half, kc), BF16),
         vmem((n_seq * half, kc), F32),
         vmem((n_seq * half, kc), BF16),
-        vmem((nz, rows, hid), BF16),
-        vmem((nz, rows, hid), F32),
-        vmem((nz, rows, hid), BF16),
-        vmem((nz, rows, hid), BF16),
-        vmem((nz, rows, hid), BF16),
-        vmem((nq, rows, hid), BF16),
+        vmem((2, nz, rows, hid // 2), BF16),
+        vmem((2, nz, rows, hid // 2), F32),
+        vmem((2, nz, rows, hid // 2), BF16),
+        vmem((2, nz, rows, hid // 2), BF16),
+        vmem((2, nz, rows, hid // 2), BF16),
+        vmem((2, nq, rows, hid // 2), BF16),
         vmem((2 * rows, cc), F32),
         vmem((nz, 2, half, cc), BF16),
         vmem((nz, 2, half, cc), BF16),
         vmem((nz, 2, half, cc), BF16),
         vmem((nz, 2, half, cc), BF16),
-        vmem((nq, half, cc), BF16),
+        vmem((2, nq, half, cc), BF16),
         vmem((phalf, vit), F32),
         vmem((2, 2, phalf, vit), BF16),
         vmem((vit // 2, hid), F32),
@@ -759,20 +790,20 @@
         vmem((2, nz, fw, hid // 2), BF16),
         vmem((nz, 2, fw, hid // 2), BF16),
         dma((qg + 10,)),
-        dma((256,)),
+        dma((320,)),
         dma((3,)),
         dma((qg,)),
         dma((n_seq,)),
-        dma((nz,)),
-        dma((nz,)),
-        dma((nz,)),
-        dma((nz,)),
+        dma((2, nz)),
+        dma((2, nz)),
+        dma((2, nz)),
+        dma((2, nz)),
         dma((nz,)),
         dma((nq,)),
         dma((nz,)),
         dma((nz,)),
         dma((2, nz)),
-        dma((2, 2)),
+        dma((nq,)),
         dma((2, 2)),
         dma((2, nz)),
         dma((nz, 2)),

time: 106 us -> 101 us (0.953); the launches traced: 106 us -> 99.5 us
  Pallas kernels: 103 us -> 96.6 us
    pallas_call x1, Pallas kernels: 103 us -> 96.6 us  [fused_on_device(): pl.pallas_call(functools.partial(fused_kernel, n_grp, n_seq), out_shape=(...]
where the time goes in v3:
time: 101 us; the launch traced here: 99.5 us
  Pallas kernels  96.6 us (96%)
  local copies, waits for them, and re-layouts  2.22 us (2%)
    pallas_call x1, Pallas kernels, fused_on_device(): pl.pallas_call(functools.partial(fused_kernel, n_grp, n_seq), out_shape=(...  96.6 us
    unnamed x3, local copies, waits for them, and re-layouts  2.22 us

profile of v3, /device:TPU:27, one launch (start us, length us, event | category | flops | bytes accessed | tf_op | source)
XLA Modules:
  0.0 99.5 jit_solution(4772663804448902917)
XLA Ops:
  0.6 96.6 %shard_map.130 = (bf16[96,1280]{1,0:T(8,128)(2,1)S(1)}, bf16[192,1280]{1,0:T(8,128)(2,1)S(1)}, f32[80,1280]{1,0:T(8,128)S(1)}) custom-call(bf16[256,4096]{1,0:T(8,128)(2,1)} %llm.1, s32[2,256]{1,0:T(2,128)} %bitcast.17, s32[1,256]{1,0:T(1,128)} %bitcast.18, s32[1,256]{1,0:T(1,128)} %bitcast.19, bf16[48,1280]{1,0:T(8,128)(2,1)} %bitcast.15, ...), custom_call_target="tpu_custom_call" | custom-call | tf_op jit(solution)/shard_map/pallas_call | solution.py:811
  97.3 0.7 copy.17
  98.0 0.8 copy.18
  98.7 0.8 copy.19

commit v4 on v3

--- a/solution.py
+++ b/solution.py
@@ -521,7 +521,6 @@
             remote(allp.at[hf, qq], allp.at[hf, qq], agy_sem.at[hf, d], y_peer).start()
 
     fc2_z(2)
-    fc2_y(3)
     def columns_of(d):
         zz = zrel(d)
         got = jnp.zeros((2 * rows, cc), F32)
@@ -560,6 +559,7 @@
         columns_of(d)
         if k:
             to_owners(near_first[k - 1])
+    fc2_y(3)
     to_owners(near_first[-1])
     def slot_table(gg):
         shape = (phalf, phalf)

time: 101 us -> 100 us (0.990); the launches traced: 99.5 us -> 99.6 us
  no operation moved by 1% of the time
where the time goes in v4:
time: 100 us; the launch traced here: 99.6 us
  Pallas kernels  96.7 us (97%)
  local copies, waits for them, and re-layouts  2.22 us (2%)
    pallas_call x1, Pallas kernels, fused_on_device(): pl.pallas_call(functools.partial(fused_kernel, n_grp, n_seq), out_shape=(...  96.7 us
    unnamed x3, local copies, waits for them, and re-layouts  2.22 us

profile of v4, /device:TPU:27, one launch (start us, length us, event | category | flops | bytes accessed | tf_op | source)
XLA Modules:
  0.0 99.6 jit_solution(10699307368936955521)
XLA Ops:
  0.6 96.7 %shard_map.130 = (bf16[96,1280]{1,0:T(8,128)(2,1)S(1)}, bf16[192,1280]{1,0:T(8,128)(2,1)S(1)}, f32[80,1280]{1,0:T(8,128)S(1)}) custom-call(bf16[256,4096]{1,0:T(8,128)(2,1)} %llm.1, s32[2,256]{1,0:T(2,128)} %bitcast.17, s32[1,256]{1,0:T(1,128)} %bitcast.18, s32[1,256]{1,0:T(1,128)} %bitcast.19, bf16[48,1280]{1,0:T(8,128)(2,1)} %bitcast.15, ...), custom_call_target="tpu_custom_call" | custom-call | tf_op jit(solution)/shard_map/pallas_call | solution.py:811
  97.3 0.7 copy.17
  98.0 0.8 copy.18
  98.8 0.8 copy.19

commit v5 on v4

--- a/solution.py
+++ b/solution.py
@@ -627,7 +627,6 @@
         to_core(far_g, k, 1)
     fc2_core(0)
     fc2_core(1)
-    fc2_core(3)
     arrive(act.at[1 - c], xw_sem.at[2])
     quarter = 2 * fw
     acts = act.reshape(2 * pslot, hid)
@@ -680,6 +679,7 @@
                     ),
                 )
 
+    fc2_core(3)
     fc2_core(2)
     for d in range(nz):
         for e in range(2):

time: 100 us -> 100 us (level)
  no operation moved by 1% of the time
where the time goes in v5:
time: 100 us; the launch traced here: 99.5 us
  Pallas kernels  96.7 us (97%)
  local copies, waits for them, and re-layouts  2.22 us (2%)
    pallas_call x1, Pallas kernels, fused_on_device(): pl.pallas_call(functools.partial(fused_kernel, n_grp, n_seq), out_shape=(...  96.7 us
    unnamed x3, local copies, waits for them, and re-layouts  2.22 us

profile of v5, /device:TPU:27, one launch (start us, length us, event | category | flops | bytes accessed | tf_op | source)
XLA Modules:
  0.0 99.5 jit_solution(824550721935836370)
XLA Ops:
  0.6 96.7 %shard_map.130 = (bf16[96,1280]{1,0:T(8,128)(2,1)S(1)}, bf16[192,1280]{1,0:T(8,128)(2,1)S(1)}, f32[80,1280]{1,0:T(8,128)S(1)}) custom-call(bf16[256,4096]{1,0:T(8,128)(2,1)} %llm.1, s32[2,256]{1,0:T(2,128)} %bitcast.17, s32[1,256]{1,0:T(1,128)} %bitcast.18, s32[1,256]{1,0:T(1,128)} %bitcast.19, bf16[48,1280]{1,0:T(8,128)(2,1)} %bitcast.15, ...), custom_call_target="tpu_custom_call" | custom-call | tf_op jit(solution)/shard_map/pallas_call | solution.py:811
  97.3 0.7 copy.17
  98.0 0.8 copy.18
  98.8 0.8 copy.19
